TPU v7x, 256 devices: a whole 4x4x8 slice. The times are simulated.
256 devices in a mesh: grp: 4 (over y), seq: 64 (over x, z, core).
Axes of the slice: x: 4, y: 4, z: 8, core: 2. Of those that a mesh axis runs over, the one named last changes fastest.
Arguments:
- queries: bfloat16 [65536, 2048], P(('grp', 'seq')), may hold values from -48 to 48
- key_rows: bfloat16 [65536, 512], P(('grp', 'seq')), may hold values from -4.5 to 4.5
- value_rows: bfloat16 [65536, 512], P(('grp', 'seq')), may hold values from -6 to 6
- segments: int32 [65536], P(('grp', 'seq')), may hold values from 0 to 30, as said below
Outputs:
- attended: bfloat16 [65536, 2048], P(('grp', 'seq'))
- log_sums: float32 [16, 65536], P(None, ('grp', 'seq'))
Inputs may be any that keep to these rules, and one draw needn't show every extreme that they name: `segments`: never falls along the sequence, starts at 0 and rises by one at each new document; the last token holds the largest value.
All inputs are finite; a program needn't handle non-finite values.
Results may differ from a plain program's by a relative error of at most 0.0035.
Values may be sent and summed in bfloat16 or wider, within the bound.
A program may use at most 192 MiB of HBM per device.

v0:
```python
import math

import jax
import jax.numpy as jnp
from jax import lax
from jax.sharding import Mesh
from jax.sharding import PartitionSpec as P

Q_HEADS = 16
KV_HEADS = 4
HEAD_DIM = 128
WINDOW = 4096
GRP_SEQ = ("grp", "seq_0", "seq_1", "seq_2")


def filled_with(array, identity):
    return jax.tree.map(
        lambda a, e: jnp.broadcast_to(jnp.asarray(e, a.dtype), a.shape), array, identity
    )


def collected_together(array, axis):
    leaves = jax.tree.leaves(array)
    order = sorted(range(len(leaves)), key=lambda k: -leaves[k].size)
    width = (1, *leaves[order[0]].shape)[-1]
    lines = [
        jnp.pad(leaves[k].reshape(-1), (0, -leaves[k].size % width)).reshape(-1, width)
        for k in order
    ]
    both, at, found = (lax.all_gather(jnp.concatenate(lines), axis), 0, {})
    for k, line in zip(order, lines):
        slab = both[:, at : at + len(line)].reshape(len(both), -1)
        found[k] = slab[:, : leaves[k].size].reshape(-1, *leaves[k].shape)
        at += len(line)
    numbers = iter(range(len(leaves)))
    return jax.tree.map(lambda _: found[next(numbers)], array)


def prefix_by_axis(array, axes, combine, identity):
    before = start = filled_with(array, identity)
    total = array
    for axis in reversed(axes):
        peers, mine = (lax.axis_size(axis), lax.axis_index(axis))
        pieces = collected_together(total, axis)
        inside, total = (start, start)
        for k in range(peers):
            passed = k < mine
            total = combine(total, jax.tree.map(lambda part: part[k], pieces))
            inside = jax.tree.map(lambda new, old: jnp.where(passed, new, old), total, inside)
        before = combine(inside, before)
    return before


def from_behind(array, axis, by):
    peers = lax.axis_size(axis)
    pairs = [(i, i + by) for i in range(peers) if 0 <= i + by < peers]
    return lax.ppermute(array, axis, pairs)


def combine(earlier, later):
    a_begin, a_first, a_last, a_start = earlier
    b_begin, b_first, b_last, b_start = later
    start = jnp.where(b_start >= 0, b_start, jnp.where(b_first != a_last, b_begin, a_start))
    merged = (a_begin, a_first, b_last, start)
    return tuple(
        (
            jnp.where(a_begin < 0, bb, jnp.where(b_begin < 0, aa, mm))
            for aa, bb, mm in zip(earlier, later, merged)
        )
    )


def find_starts(segments, offset, tok):
    change = segments[1:] != segments[:-1]
    inner_pos = offset + jnp.arange(1, tok, dtype=jnp.int32)
    inner = jnp.max(jnp.where(change, inner_pos, -1))
    mine = (offset, segments[0], segments[tok - 1], inner)
    minus = jnp.int32(-1)
    prefix = prefix_by_axis(mine, GRP_SEQ, combine, (minus, minus, minus, minus))
    p_begin, p_first, p_last, p_start = prefix
    carried = jnp.where(p_begin < 0, 0, jnp.where(p_start >= 0, p_start, p_begin)).astype(jnp.int32)
    head_flag = (p_begin >= 0) & (segments[0] != p_last)
    flags = jnp.concatenate([head_flag[None], change])
    marks = jnp.where(flags, offset + jnp.arange(tok, dtype=jnp.int32), -1)
    return jnp.maximum(lax.cummax(marks, axis=0), carried)


def attend(state, q_heads, key_block, value_block, key_first, positions, lower):
    length = key_block.shape[0]
    k_heads = key_block.reshape(length, KV_HEADS, HEAD_DIM)
    v_heads = value_block.reshape(length, KV_HEADS, HEAD_DIM)
    scale = 1.0 / math.sqrt(HEAD_DIM)
    top, total, summed = state
    scores = (
        jnp.einsum("tkgd,lkd->kgtl", q_heads, k_heads, preferred_element_type=jnp.float32) * scale
    )
    key_pos = key_first + jnp.arange(length, dtype=jnp.int32)
    allowed = (key_pos[None, :] >= lower[:, None]) & (key_pos[None, :] <= positions[:, None])
    masked = jnp.where(allowed, scores, -1e30)
    top_new = jnp.maximum(top, jnp.max(masked, axis=-1))
    expo = jnp.where(allowed, jnp.exp(masked - top_new[..., None]), 0.0)
    factor = jnp.exp(top - top_new)
    total_new = total * factor + jnp.sum(expo, axis=-1)
    weights = expo.astype(jnp.bfloat16)
    update = jnp.einsum("kgtl,lkd->tkgd", weights, v_heads, preferred_element_type=jnp.float32)
    summed_new = summed * jnp.transpose(factor, (2, 0, 1))[..., None] + update
    return (top_new, total_new, summed_new)


def on_device(queries, key_rows, value_rows, segments):
    tok = queries.shape[0]
    group = Q_HEADS // KV_HEADS
    device = lax.axis_index(GRP_SEQ)
    offset = device * tok
    starts = find_starts(segments, offset, tok)
    positions = offset + jnp.arange(tok, dtype=jnp.int32)
    lower = jnp.maximum(starts, positions - WINDOW + 1)
    q_heads = queries.reshape(tok, KV_HEADS, group, HEAD_DIM)
    state = (
        jnp.full((KV_HEADS, group, tok), -1e30, jnp.float32),
        jnp.zeros((KV_HEADS, group, tok), jnp.float32),
        jnp.zeros((tok, KV_HEADS, group, HEAD_DIM), jnp.float32),
    )
    state = attend(state, q_heads, key_rows, value_rows, offset, positions, lower)
    reach = (WINDOW - 1) // tok + 1

    def one_step(turn, carry):
        blocks, current = carry
        blocks = from_behind((blocks[0], blocks[1]), GRP_SEQ, 1)
        key_first = offset - (turn + 1) * tok
        current = attend(current, q_heads, blocks[0], blocks[1], key_first, positions, lower)
        return (blocks, current)

    final = lax.fori_loop(0, reach, one_step, ((key_rows, value_rows), state))
    state = final[1]
    top, total, summed = state
    attended = (
        (summed / jnp.transpose(total, (2, 0, 1))[..., None])
        .reshape(tok, Q_HEADS * HEAD_DIM)
        .astype(jnp.bfloat16)
    )
    log_sums = (top + jnp.log(total)).reshape(Q_HEADS, tok)
    return (attended, log_sums)


def solution(mesh):
    split = Mesh(
        mesh.devices.reshape(mesh.shape["grp"], 4, 8, 2), ("grp", "seq_0", "seq_1", "seq_2")
    )
    placed = (P(GRP_SEQ, None), P(GRP_SEQ, None), P(GRP_SEQ, None), P(GRP_SEQ))
    return jax.shard_map(
        on_device,
        mesh=split,
        in_specs=placed,
        out_specs=(P(GRP_SEQ, None), P(None, GRP_SEQ)),
        check_vma=False,
    )
```

profile of v0, /device:TPU:8, one launch (start us, length us, event | category | flops | bytes accessed | tf_op | source)
XLA Modules:
  0.0 472.1 jit_solution(119159346198983746)
XLA Ops:
  5.4 2.0 fusion.36
  22.6 16.1 %all-reduce.1 = s32[32]{0:T(128)S(1)} all-reduce(s32[32]{0:T(128)S(1)} %fusion.37), channel_id=3, replica_groups=mesh['grp'=4,'seq_0'=4,'seq_1'=8,'seq_2'=2] {'seq_1'}, use_global_device_ids=true, to_apply=%add.1 | all-reduce | flops 32 | bytes 256
  90.9 8.9 %all-reduce.2 = s32[16]{0:T(128)S(1)} all-reduce(s32[16]{0:T(128)S(1)} %fusion.38), channel_id=4, replica_groups=mesh['grp'=4,'seq_0'=4,'seq_1'=8,'seq_2'=2] {'seq_0'}, use_global_device_ids=true, to_apply=%add.2 | all-reduce | flops 16 | bytes 128
  130.2 8.2 %all-reduce.3 = s32[16]{0:T(128)S(1)} all-reduce(s32[16]{0:T(128)S(1)} %fusion.39), channel_id=5, replica_groups=mesh['grp'=4,'seq_0'=4,'seq_1'=8,'seq_2'=2] {'grp'}, use_global_device_ids=true, to_apply=%add.3 | all-reduce | flops 16 | bytes 128
  173.3 5.3 %bitcast_add_fusion.1 = f32[256,4,4,128]{3,0,2,1:T(8,128)} fusion(f32[4,256,256,4]{2,1,3,0:T(8,128)} %copy-done, f32[4,4,256]{2,1,0:T(4,128)S(1)} %broadcast_maximum_fusion, pred[256,256]{0,1:T(8,128)(4,1)S(1)} %compare_and_fusion.1, f32[256,4,4]{0,2,1:T(4,128)S(1)} %get-tuple-element.256, bf16[256,4,128,1]{2,1,0,3:T(4,128)(2,1)S(1)} %bitcast.218), kind=kOutput, calls=%fused_computation.28 | convolution fusion | flops 274202624 | bytes 6651904 | tf_op jit(solution)/shard_map/kgtl,lkd->tkgd/dot_general | solution.py:105
  179.6 287.6 %while.23 = (s32[]{:T(128)}, bf16[256,512]{0,1:T(8,128)(2,1)S(1)}, bf16[256,512]{0,1:T(8,128)(2,1)S(1)}, f32[4,4,256]{2,1,0:T(4,128)S(1)}, f32[4,4,256]{2,1,0:T(...) while((s32[]{:T(128)}, bf16[256,512]{0,1:T(8,128)(2,1)S(1)}, ...), condition=%wide.region_8.9_spmd.clone.clone, body=%wide.region_5.8_spmd.clone.clone.sunk | while | flops 551760384 | bytes 38802708 | solution.py:134
  179.6 1.9 collective-permute-start
  181.5 3.0 collective-permute-start.1
  184.7 6.8 %collective-permute-done = bf16[256,512]{0,1:T(8,128)(2,1)S(1)} collective-permute-done((bf16[256,512]{0,1:T(8,128)(2,1)S(1)}, bf16[256,512]{0,1:T(8,128)(2,1)S(1)}, u32[]{:S(2)}, u32[]{:S(2)}) %collective-permute-start) | collective-permute-done | bytes 262176 | tf_op jit(solution)/shard_map/while/body/eval_jaxpr/ppermute | solution.py:57
  194.3 1.9 bitcast_add_fusion.3
  199.5 1.9 collective-permute-start.1
  201.6 7.9 %collective-permute-done = bf16[256,512]{0,1:T(8,128)(2,1)S(1)} collective-permute-done((bf16[256,512]{0,1:T(8,128)(2,1)S(1)}, bf16[256,512]{0,1:T(8,128)(2,1)S(1)}, u32[]{:S(2)}, u32[]{:S(2)}) %collective-permute-start) | collective-permute-done | bytes 262176 | tf_op jit(solution)/shard_map/while/body/eval_jaxpr/ppermute | solution.py:57
  212.3 1.9 bitcast_add_fusion.3
  217.5 1.9 collective-permute-start.1
  219.5 7.9 %collective-permute-done = bf16[256,512]{0,1:T(8,128)(2,1)S(1)} collective-permute-done((bf16[256,512]{0,1:T(8,128)(2,1)S(1)}, bf16[256,512]{0,1:T(8,128)(2,1)S(1)}, u32[]{:S(2)}, u32[]{:S(2)}) %collective-permute-start) | collective-permute-done | bytes 262176 | tf_op jit(solution)/shard_map/while/body/eval_jaxpr/ppermute | solution.py:57
  230.3 1.9 bitcast_add_fusion.3
  235.4 1.9 collective-permute-start.1
  237.5 7.9 %collective-permute-done = bf16[256,512]{0,1:T(8,128)(2,1)S(1)} collective-permute-done((bf16[256,512]{0,1:T(8,128)(2,1)S(1)}, bf16[256,512]{0,1:T(8,128)(2,1)S(1)}, u32[]{:S(2)}, u32[]{:S(2)}) %collective-permute-start) | collective-permute-done | bytes 262176 | tf_op jit(solution)/shard_map/while/body/eval_jaxpr/ppermute | solution.py:57
  248.2 1.9 bitcast_add_fusion.3
  255.5 7.9 %collective-permute-done = bf16[256,512]{0,1:T(8,128)(2,1)S(1)} collective-permute-done((bf16[256,512]{0,1:T(8,128)(2,1)S(1)}, bf16[256,512]{0,1:T(8,128)(2,1)S(1)}, u32[]{:S(2)}, u32[]{:S(2)}) %collective-permute-start) | collective-permute-done | bytes 262176 | tf_op jit(solution)/shard_map/while/body/eval_jaxpr/ppermute | solution.py:57
  266.2 1.9 bitcast_add_fusion.3
  273.5 7.9 %collective-permute-done = bf16[256,512]{0,1:T(8,128)(2,1)S(1)} collective-permute-done((bf16[256,512]{0,1:T(8,128)(2,1)S(1)}, bf16[256,512]{0,1:T(8,128)(2,1)S(1)}, u32[]{:S(2)}, u32[]{:S(2)}) %collective-permute-start) | collective-permute-done | bytes 262176 | tf_op jit(solution)/shard_map/while/body/eval_jaxpr/ppermute | solution.py:57
  284.2 1.9 bitcast_add_fusion.3
  289.3 1.9 collective-permute-start.1
  291.4 7.9 %collective-permute-done = bf16[256,512]{0,1:T(8,128)(2,1)S(1)} collective-permute-done((bf16[256,512]{0,1:T(8,128)(2,1)S(1)}, bf16[256,512]{0,1:T(8,128)(2,1)S(1)}, u32[]{:S(2)}, u32[]{:S(2)}) %collective-permute-start) | collective-permute-done | bytes 262176 | tf_op jit(solution)/shard_map/while/body/eval_jaxpr/ppermute | solution.py:57
  302.1 1.9 bitcast_add_fusion.3
  309.4 7.9 %collective-permute-done = bf16[256,512]{0,1:T(8,128)(2,1)S(1)} collective-permute-done((bf16[256,512]{0,1:T(8,128)(2,1)S(1)}, bf16[256,512]{0,1:T(8,128)(2,1)S(1)}, u32[]{:S(2)}, u32[]{:S(2)}) %collective-permute-start) | collective-permute-done | bytes 262176 | tf_op jit(solution)/shard_map/while/body/eval_jaxpr/ppermute | solution.py:57
  320.1 1.9 bitcast_add_fusion.3
  327.4 7.9 %collective-permute-done = bf16[256,512]{0,1:T(8,128)(2,1)S(1)} collective-permute-done((bf16[256,512]{0,1:T(8,128)(2,1)S(1)}, bf16[256,512]{0,1:T(8,128)(2,1)S(1)}, u32[]{:S(2)}, u32[]{:S(2)}) %collective-permute-start) | collective-permute-done | bytes 262176 | tf_op jit(solution)/shard_map/while/body/eval_jaxpr/ppermute | solution.py:57
  338.1 1.9 bitcast_add_fusion.3
  343.3 1.9 collective-permute-start.1
  345.3 7.9 %collective-permute-done = bf16[256,512]{0,1:T(8,128)(2,1)S(1)} collective-permute-done((bf16[256,512]{0,1:T(8,128)(2,1)S(1)}, bf16[256,512]{0,1:T(8,128)(2,1)S(1)}, u32[]{:S(2)}, u32[]{:S(2)}) %collective-permute-start) | collective-permute-done | bytes 262176 | tf_op jit(solution)/shard_map/while/body/eval_jaxpr/ppermute | solution.py:57
  356.1 1.9 bitcast_add_fusion.3
  363.3 7.9 %collective-permute-done = bf16[256,512]{0,1:T(8,128)(2,1)S(1)} collective-permute-done((bf16[256,512]{0,1:T(8,128)(2,1)S(1)}, bf16[256,512]{0,1:T(8,128)(2,1)S(1)}, u32[]{:S(2)}, u32[]{:S(2)}) %collective-permute-start) | collective-permute-done | bytes 262176 | tf_op jit(solution)/shard_map/while/body/eval_jaxpr/ppermute | solution.py:57
  374.0 1.9 bitcast_add_fusion.3
  381.3 7.9 %collective-permute-done = bf16[256,512]{0,1:T(8,128)(2,1)S(1)} collective-permute-done((bf16[256,512]{0,1:T(8,128)(2,1)S(1)}, bf16[256,512]{0,1:T(8,128)(2,1)S(1)}, u32[]{:S(2)}, u32[]{:S(2)}) %collective-permute-start) | collective-permute-done | bytes 262176 | tf_op jit(solution)/shard_map/while/body/eval_jaxpr/ppermute | solution.py:57
  392.0 1.9 bitcast_add_fusion.3
  397.2 1.9 collective-permute-start.1
  399.2 7.9 %collective-permute-done = bf16[256,512]{0,1:T(8,128)(2,1)S(1)} collective-permute-done((bf16[256,512]{0,1:T(8,128)(2,1)S(1)}, bf16[256,512]{0,1:T(8,128)(2,1)S(1)}, u32[]{:S(2)}, u32[]{:S(2)}) %collective-permute-start) | collective-permute-done | bytes 262176 | tf_op jit(solution)/shard_map/while/body/eval_jaxpr/ppermute | solution.py:57
  410.0 1.9 bitcast_add_fusion.3
  417.2 7.9 %collective-permute-done = bf16[256,512]{0,1:T(8,128)(2,1)S(1)} collective-permute-done((bf16[256,512]{0,1:T(8,128)(2,1)S(1)}, bf16[256,512]{0,1:T(8,128)(2,1)S(1)}, u32[]{:S(2)}, u32[]{:S(2)}) %collective-permute-start) | collective-permute-done | bytes 262176 | tf_op jit(solution)/shard_map/while/body/eval_jaxpr/ppermute | solution.py:57
  427.9 1.9 bitcast_add_fusion.3
  435.2 7.9 %collective-permute-done = bf16[256,512]{0,1:T(8,128)(2,1)S(1)} collective-permute-done((bf16[256,512]{0,1:T(8,128)(2,1)S(1)}, bf16[256,512]{0,1:T(8,128)(2,1)S(1)}, u32[]{:S(2)}, u32[]{:S(2)}) %collective-permute-start) | collective-permute-done | bytes 262176 | tf_op jit(solution)/shard_map/while/body/eval_jaxpr/ppermute | solution.py:57
  445.9 1.9 bitcast_add_fusion.3
  451.1 1.9 collective-permute-start.1
  453.2 7.9 %collective-permute-done = bf16[256,512]{0,1:T(8,128)(2,1)S(1)} collective-permute-done((bf16[256,512]{0,1:T(8,128)(2,1)S(1)}, bf16[256,512]{0,1:T(8,128)(2,1)S(1)}, u32[]{:S(2)}, u32[]{:S(2)}) %collective-permute-start) | collective-permute-done | bytes 262176 | tf_op jit(solution)/shard_map/while/body/eval_jaxpr/ppermute | solution.py:57
  463.9 1.9 bitcast_add_fusion.3
  467.8 1.9 divide_convert_fusion
  (298 shorter events, 136.7 us)
Async XLA Ops:
  169.4 3.8 copy-start.4
  173.3 6.0 %copy-start.3 = (bf16[256,512]{1,0:T(8,128)(2,1)S(1)}, bf16[256,512]{1,0:T(8,128)(2,1)}, u32[]{:S(2)}) copy-start(bf16[256,512]{1,0:T(8,128)(2,1)} %param.7) | copy-start | bytes 786436
  179.6 11.9 %collective-permute-start = (bf16[256,512]{0,1:T(8,128)(2,1)S(1)}, bf16[256,512]{0,1:T(8,128)(2,1)S(1)}, u32[]{:S(2)}, u32[]{:S(2)}) collective-permute-start(bf16[256,512]{0,1:T(8,128)(2,1)S(1)} %get-tuple-element.412), channel_id=1, source_target_pairs={{0,1},{1,2},{2,3},{3,4},{4,5},{5,6},{6,7},{7,8},{8,9},{9,10},{10,1... | collective-permute-start | bytes 786440 | tf_op jit(solution)/shard_map/while/body/eval_jaxpr/ppermute | solution.py:57
  181.5 12.8 %collective-permute-start.1 = (bf16[256,512]{0,1:T(8,128)(2,1)S(1)}, bf16[256,512]{0,1:T(8,128)(2,1)S(1)}, u32[]{:S(2)}, u32[]{:S(2)}) collective-permute-start(bf16[256,512]{0,1:T(8,128)(2,1)S(1)} %get-tuple-element.413), channel_id=1, source_target_pairs={{0,1},{1,2},{2,3},{3,4},{4,5},{5,6},{6,7},{7,8},{8,9},{9,10},{10,1... | collective-permute-start | bytes 786440 | tf_op jit(solution)/shard_map/while/body/eval_jaxpr/ppermute | solution.py:57
  191.5 2.8 copy-start.1
  197.6 11.9 %collective-permute-start = (bf16[256,512]{0,1:T(8,128)(2,1)S(1)}, bf16[256,512]{0,1:T(8,128)(2,1)S(1)}, u32[]{:S(2)}, u32[]{:S(2)}) collective-permute-start(bf16[256,512]{0,1:T(8,128)(2,1)S(1)} %get-tuple-element.412), channel_id=1, source_target_pairs={{0,1},{1,2},{2,3},{3,4},{4,5},{5,6},{6,7},{7,8},{8,9},{9,10},{10,1... | collective-permute-start | bytes 786440 | tf_op jit(solution)/shard_map/while/body/eval_jaxpr/ppermute | solution.py:57
  199.5 12.8 %collective-permute-start.1 = (bf16[256,512]{0,1:T(8,128)(2,1)S(1)}, bf16[256,512]{0,1:T(8,128)(2,1)S(1)}, u32[]{:S(2)}, u32[]{:S(2)}) collective-permute-start(bf16[256,512]{0,1:T(8,128)(2,1)S(1)} %get-tuple-element.413), channel_id=1, source_target_pairs={{0,1},{1,2},{2,3},{3,4},{4,5},{5,6},{6,7},{7,8},{8,9},{9,10},{10,1... | collective-permute-start | bytes 786440 | tf_op jit(solution)/shard_map/while/body/eval_jaxpr/ppermute | solution.py:57
  209.5 2.8 copy-start.1
  215.6 11.9 %collective-permute-start = (bf16[256,512]{0,1:T(8,128)(2,1)S(1)}, bf16[256,512]{0,1:T(8,128)(2,1)S(1)}, u32[]{:S(2)}, u32[]{:S(2)}) collective-permute-start(bf16[256,512]{0,1:T(8,128)(2,1)S(1)} %get-tuple-element.412), channel_id=1, source_target_pairs={{0,1},{1,2},{2,3},{3,4},{4,5},{5,6},{6,7},{7,8},{8,9},{9,10},{10,1... | collective-permute-start | bytes 786440 | tf_op jit(solution)/shard_map/while/body/eval_jaxpr/ppermute | solution.py:57
  217.5 12.8 %collective-permute-start.1 = (bf16[256,512]{0,1:T(8,128)(2,1)S(1)}, bf16[256,512]{0,1:T(8,128)(2,1)S(1)}, u32[]{:S(2)}, u32[]{:S(2)}) collective-permute-start(bf16[256,512]{0,1:T(8,128)(2,1)S(1)} %get-tuple-element.413), channel_id=1, source_target_pairs={{0,1},{1,2},{2,3},{3,4},{4,5},{5,6},{6,7},{7,8},{8,9},{9,10},{10,1... | collective-permute-start | bytes 786440 | tf_op jit(solution)/shard_map/while/body/eval_jaxpr/ppermute | solution.py:57
  227.4 2.8 copy-start.1
  233.5 11.9 %collective-permute-start = (bf16[256,512]{0,1:T(8,128)(2,1)S(1)}, bf16[256,512]{0,1:T(8,128)(2,1)S(1)}, u32[]{:S(2)}, u32[]{:S(2)}) collective-permute-start(bf16[256,512]{0,1:T(8,128)(2,1)S(1)} %get-tuple-element.412), channel_id=1, source_target_pairs={{0,1},{1,2},{2,3},{3,4},{4,5},{5,6},{6,7},{7,8},{8,9},{9,10},{10,1... | collective-permute-start | bytes 786440 | tf_op jit(solution)/shard_map/while/body/eval_jaxpr/ppermute | solution.py:57
  235.4 12.8 %collective-permute-start.1 = (bf16[256,512]{0,1:T(8,128)(2,1)S(1)}, bf16[256,512]{0,1:T(8,128)(2,1)S(1)}, u32[]{:S(2)}, u32[]{:S(2)}) collective-permute-start(bf16[256,512]{0,1:T(8,128)(2,1)S(1)} %get-tuple-element.413), channel_id=1, source_target_pairs={{0,1},{1,2},{2,3},{3,4},{4,5},{5,6},{6,7},{7,8},{8,9},{9,10},{10,1... | collective-permute-start | bytes 786440 | tf_op jit(solution)/shard_map/while/body/eval_jaxpr/ppermute | solution.py:57
  245.4 2.8 copy-start.1
  251.5 11.9 %collective-permute-start = (bf16[256,512]{0,1:T(8,128)(2,1)S(1)}, bf16[256,512]{0,1:T(8,128)(2,1)S(1)}, u32[]{:S(2)}, u32[]{:S(2)}) collective-permute-start(bf16[256,512]{0,1:T(8,128)(2,1)S(1)} %get-tuple-element.412), channel_id=1, source_target_pairs={{0,1},{1,2},{2,3},{3,4},{4,5},{5,6},{6,7},{7,8},{8,9},{9,10},{10,1... | collective-permute-start | bytes 786440 | tf_op jit(solution)/shard_map/while/body/eval_jaxpr/ppermute | solution.py:57
  253.4 12.8 %collective-permute-start.1 = (bf16[256,512]{0,1:T(8,128)(2,1)S(1)}, bf16[256,512]{0,1:T(8,128)(2,1)S(1)}, u32[]{:S(2)}, u32[]{:S(2)}) collective-permute-start(bf16[256,512]{0,1:T(8,128)(2,1)S(1)} %get-tuple-element.413), channel_id=1, source_target_pairs={{0,1},{1,2},{2,3},{3,4},{4,5},{5,6},{6,7},{7,8},{8,9},{9,10},{10,1... | collective-permute-start | bytes 786440 | tf_op jit(solution)/shard_map/while/body/eval_jaxpr/ppermute | solution.py:57
  263.4 2.8 copy-start.1
  269.5 11.9 %collective-permute-start = (bf16[256,512]{0,1:T(8,128)(2,1)S(1)}, bf16[256,512]{0,1:T(8,128)(2,1)S(1)}, u32[]{:S(2)}, u32[]{:S(2)}) collective-permute-start(bf16[256,512]{0,1:T(8,128)(2,1)S(1)} %get-tuple-element.412), channel_id=1, source_target_pairs={{0,1},{1,2},{2,3},{3,4},{4,5},{5,6},{6,7},{7,8},{8,9},{9,10},{10,1... | collective-permute-start | bytes 786440 | tf_op jit(solution)/shard_map/while/body/eval_jaxpr/ppermute | solution.py:57
  271.4 12.8 %collective-permute-start.1 = (bf16[256,512]{0,1:T(8,128)(2,1)S(1)}, bf16[256,512]{0,1:T(8,128)(2,1)S(1)}, u32[]{:S(2)}, u32[]{:S(2)}) collective-permute-start(bf16[256,512]{0,1:T(8,128)(2,1)S(1)} %get-tuple-element.413), channel_id=1, source_target_pairs={{0,1},{1,2},{2,3},{3,4},{4,5},{5,6},{6,7},{7,8},{8,9},{9,10},{10,1... | collective-permute-start | bytes 786440 | tf_op jit(solution)/shard_map/while/body/eval_jaxpr/ppermute | solution.py:57
  281.4 2.8 copy-start.1
  287.4 11.9 %collective-permute-start = (bf16[256,512]{0,1:T(8,128)(2,1)S(1)}, bf16[256,512]{0,1:T(8,128)(2,1)S(1)}, u32[]{:S(2)}, u32[]{:S(2)}) collective-permute-start(bf16[256,512]{0,1:T(8,128)(2,1)S(1)} %get-tuple-element.412), channel_id=1, source_target_pairs={{0,1},{1,2},{2,3},{3,4},{4,5},{5,6},{6,7},{7,8},{8,9},{9,10},{10,1... | collective-permute-start | bytes 786440 | tf_op jit(solution)/shard_map/while/body/eval_jaxpr/ppermute | solution.py:57
  289.3 12.8 %collective-permute-start.1 = (bf16[256,512]{0,1:T(8,128)(2,1)S(1)}, bf16[256,512]{0,1:T(8,128)(2,1)S(1)}, u32[]{:S(2)}, u32[]{:S(2)}) collective-permute-start(bf16[256,512]{0,1:T(8,128)(2,1)S(1)} %get-tuple-element.413), channel_id=1, source_target_pairs={{0,1},{1,2},{2,3},{3,4},{4,5},{5,6},{6,7},{7,8},{8,9},{9,10},{10,1... | collective-permute-start | bytes 786440 | tf_op jit(solution)/shard_map/while/body/eval_jaxpr/ppermute | solution.py:57
  299.3 2.8 copy-start.1
  305.4 11.9 %collective-permute-start = (bf16[256,512]{0,1:T(8,128)(2,1)S(1)}, bf16[256,512]{0,1:T(8,128)(2,1)S(1)}, u32[]{:S(2)}, u32[]{:S(2)}) collective-permute-start(bf16[256,512]{0,1:T(8,128)(2,1)S(1)} %get-tuple-element.412), channel_id=1, source_target_pairs={{0,1},{1,2},{2,3},{3,4},{4,5},{5,6},{6,7},{7,8},{8,9},{9,10},{10,1... | collective-permute-start | bytes 786440 | tf_op jit(solution)/shard_map/while/body/eval_jaxpr/ppermute | solution.py:57
  307.3 12.8 %collective-permute-start.1 = (bf16[256,512]{0,1:T(8,128)(2,1)S(1)}, bf16[256,512]{0,1:T(8,128)(2,1)S(1)}, u32[]{:S(2)}, u32[]{:S(2)}) collective-permute-start(bf16[256,512]{0,1:T(8,128)(2,1)S(1)} %get-tuple-element.413), channel_id=1, source_target_pairs={{0,1},{1,2},{2,3},{3,4},{4,5},{5,6},{6,7},{7,8},{8,9},{9,10},{10,1... | collective-permute-start | bytes 786440 | tf_op jit(solution)/shard_map/while/body/eval_jaxpr/ppermute | solution.py:57
  317.3 2.8 copy-start.1
  323.4 11.9 %collective-permute-start = (bf16[256,512]{0,1:T(8,128)(2,1)S(1)}, bf16[256,512]{0,1:T(8,128)(2,1)S(1)}, u32[]{:S(2)}, u32[]{:S(2)}) collective-permute-start(bf16[256,512]{0,1:T(8,128)(2,1)S(1)} %get-tuple-element.412), channel_id=1, source_target_pairs={{0,1},{1,2},{2,3},{3,4},{4,5},{5,6},{6,7},{7,8},{8,9},{9,10},{10,1... | collective-permute-start | bytes 786440 | tf_op jit(solution)/shard_map/while/body/eval_jaxpr/ppermute | solution.py:57
  325.3 12.8 %collective-permute-start.1 = (bf16[256,512]{0,1:T(8,128)(2,1)S(1)}, bf16[256,512]{0,1:T(8,128)(2,1)S(1)}, u32[]{:S(2)}, u32[]{:S(2)}) collective-permute-start(bf16[256,512]{0,1:T(8,128)(2,1)S(1)} %get-tuple-element.413), channel_id=1, source_target_pairs={{0,1},{1,2},{2,3},{3,4},{4,5},{5,6},{6,7},{7,8},{8,9},{9,10},{10,1... | collective-permute-start | bytes 786440 | tf_op jit(solution)/shard_map/while/body/eval_jaxpr/ppermute | solution.py:57
  335.3 2.8 copy-start.1
  341.3 11.9 %collective-permute-start = (bf16[256,512]{0,1:T(8,128)(2,1)S(1)}, bf16[256,512]{0,1:T(8,128)(2,1)S(1)}, u32[]{:S(2)}, u32[]{:S(2)}) collective-permute-start(bf16[256,512]{0,1:T(8,128)(2,1)S(1)} %get-tuple-element.412), channel_id=1, source_target_pairs={{0,1},{1,2},{2,3},{3,4},{4,5},{5,6},{6,7},{7,8},{8,9},{9,10},{10,1... | collective-permute-start | bytes 786440 | tf_op jit(solution)/shard_map/while/body/eval_jaxpr/ppermute | solution.py:57
  343.3 12.8 %collective-permute-start.1 = (bf16[256,512]{0,1:T(8,128)(2,1)S(1)}, bf16[256,512]{0,1:T(8,128)(2,1)S(1)}, u32[]{:S(2)}, u32[]{:S(2)}) collective-permute-start(bf16[256,512]{0,1:T(8,128)(2,1)S(1)} %get-tuple-element.413), channel_id=1, source_target_pairs={{0,1},{1,2},{2,3},{3,4},{4,5},{5,6},{6,7},{7,8},{8,9},{9,10},{10,1... | collective-permute-start | bytes 786440 | tf_op jit(solution)/shard_map/while/body/eval_jaxpr/ppermute | solution.py:57
  353.2 2.8 copy-start.1
  359.3 11.9 %collective-permute-start = (bf16[256,512]{0,1:T(8,128)(2,1)S(1)}, bf16[256,512]{0,1:T(8,128)(2,1)S(1)}, u32[]{:S(2)}, u32[]{:S(2)}) collective-permute-start(bf16[256,512]{0,1:T(8,128)(2,1)S(1)} %get-tuple-element.412), channel_id=1, source_target_pairs={{0,1},{1,2},{2,3},{3,4},{4,5},{5,6},{6,7},{7,8},{8,9},{9,10},{10,1... | collective-permute-start | bytes 786440 | tf_op jit(solution)/shard_map/while/body/eval_jaxpr/ppermute | solution.py:57
  361.2 12.8 %collective-permute-start.1 = (bf16[256,512]{0,1:T(8,128)(2,1)S(1)}, bf16[256,512]{0,1:T(8,128)(2,1)S(1)}, u32[]{:S(2)}, u32[]{:S(2)}) collective-permute-start(bf16[256,512]{0,1:T(8,128)(2,1)S(1)} %get-tuple-element.413), channel_id=1, source_target_pairs={{0,1},{1,2},{2,3},{3,4},{4,5},{5,6},{6,7},{7,8},{8,9},{9,10},{10,1... | collective-permute-start | bytes 786440 | tf_op jit(solution)/shard_map/while/body/eval_jaxpr/ppermute | solution.py:57
  371.2 2.8 copy-start.1
  377.3 11.9 %collective-permute-start = (bf16[256,512]{0,1:T(8,128)(2,1)S(1)}, bf16[256,512]{0,1:T(8,128)(2,1)S(1)}, u32[]{:S(2)}, u32[]{:S(2)}) collective-permute-start(bf16[256,512]{0,1:T(8,128)(2,1)S(1)} %get-tuple-element.412), channel_id=1, source_target_pairs={{0,1},{1,2},{2,3},{3,4},{4,5},{5,6},{6,7},{7,8},{8,9},{9,10},{10,1... | collective-permute-start | bytes 786440 | tf_op jit(solution)/shard_map/while/body/eval_jaxpr/ppermute | solution.py:57
  379.2 12.8 %collective-permute-start.1 = (bf16[256,512]{0,1:T(8,128)(2,1)S(1)}, bf16[256,512]{0,1:T(8,128)(2,1)S(1)}, u32[]{:S(2)}, u32[]{:S(2)}) collective-permute-start(bf16[256,512]{0,1:T(8,128)(2,1)S(1)} %get-tuple-element.413), channel_id=1, source_target_pairs={{0,1},{1,2},{2,3},{3,4},{4,5},{5,6},{6,7},{7,8},{8,9},{9,10},{10,1... | collective-permute-start | bytes 786440 | tf_op jit(solution)/shard_map/while/body/eval_jaxpr/ppermute | solution.py:57
  389.2 2.8 copy-start.1
  395.3 11.9 %collective-permute-start = (bf16[256,512]{0,1:T(8,128)(2,1)S(1)}, bf16[256,512]{0,1:T(8,128)(2,1)S(1)}, u32[]{:S(2)}, u32[]{:S(2)}) collective-permute-start(bf16[256,512]{0,1:T(8,128)(2,1)S(1)} %get-tuple-element.412), channel_id=1, source_target_pairs={{0,1},{1,2},{2,3},{3,4},{4,5},{5,6},{6,7},{7,8},{8,9},{9,10},{10,1... | collective-permute-start | bytes 786440 | tf_op jit(solution)/shard_map/while/body/eval_jaxpr/ppermute | solution.py:57
  397.2 12.8 %collective-permute-start.1 = (bf16[256,512]{0,1:T(8,128)(2,1)S(1)}, bf16[256,512]{0,1:T(8,128)(2,1)S(1)}, u32[]{:S(2)}, u32[]{:S(2)}) collective-permute-start(bf16[256,512]{0,1:T(8,128)(2,1)S(1)} %get-tuple-element.413), channel_id=1, source_target_pairs={{0,1},{1,2},{2,3},{3,4},{4,5},{5,6},{6,7},{7,8},{8,9},{9,10},{10,1... | collective-permute-start | bytes 786440 | tf_op jit(solution)/shard_map/while/body/eval_jaxpr/ppermute | solution.py:57
  413.2 11.9 %collective-permute-start = (bf16[256,512]{0,1:T(8,128)(2,1)S(1)}, bf16[256,512]{0,1:T(8,128)(2,1)S(1)}, u32[]{:S(2)}, u32[]{:S(2)}) collective-permute-start(bf16[256,512]{0,1:T(8,128)(2,1)S(1)} %get-tuple-element.412), channel_id=1, source_target_pairs={{0,1},{1,2},{2,3},{3,4},{4,5},{5,6},{6,7},{7,8},{8,9},{9,10},{10,1... | collective-permute-start | bytes 786440 | tf_op jit(solution)/shard_map/while/body/eval_jaxpr/ppermute | solution.py:57
  415.1 12.8 %collective-permute-start.1 = (bf16[256,512]{0,1:T(8,128)(2,1)S(1)}, bf16[256,512]{0,1:T(8,128)(2,1)S(1)}, u32[]{:S(2)}, u32[]{:S(2)}) collective-permute-start(bf16[256,512]{0,1:T(8,128)(2,1)S(1)} %get-tuple-element.413), channel_id=1, source_target_pairs={{0,1},{1,2},{2,3},{3,4},{4,5},{5,6},{6,7},{7,8},{8,9},{9,10},{10,1... | collective-permute-start | bytes 786440 | tf_op jit(solution)/shard_map/while/body/eval_jaxpr/ppermute | solution.py:57
  425.1 2.8 copy-start.1
  431.2 11.9 %collective-permute-start = (bf16[256,512]{0,1:T(8,128)(2,1)S(1)}, bf16[256,512]{0,1:T(8,128)(2,1)S(1)}, u32[]{:S(2)}, u32[]{:S(2)}) collective-permute-start(bf16[256,512]{0,1:T(8,128)(2,1)S(1)} %get-tuple-element.412), channel_id=1, source_target_pairs={{0,1},{1,2},{2,3},{3,4},{4,5},{5,6},{6,7},{7,8},{8,9},{9,10},{10,1... | collective-permute-start | bytes 786440 | tf_op jit(solution)/shard_map/while/body/eval_jaxpr/ppermute | solution.py:57
  433.1 12.8 %collective-permute-start.1 = (bf16[256,512]{0,1:T(8,128)(2,1)S(1)}, bf16[256,512]{0,1:T(8,128)(2,1)S(1)}, u32[]{:S(2)}, u32[]{:S(2)}) collective-permute-start(bf16[256,512]{0,1:T(8,128)(2,1)S(1)} %get-tuple-element.413), channel_id=1, source_target_pairs={{0,1},{1,2},{2,3},{3,4},{4,5},{5,6},{6,7},{7,8},{8,9},{9,10},{10,1... | collective-permute-start | bytes 786440 | tf_op jit(solution)/shard_map/while/body/eval_jaxpr/ppermute | solution.py:57
  443.1 2.8 copy-start.1
  449.2 11.9 %collective-permute-start = (bf16[256,512]{0,1:T(8,128)(2,1)S(1)}, bf16[256,512]{0,1:T(8,128)(2,1)S(1)}, u32[]{:S(2)}, u32[]{:S(2)}) collective-permute-start(bf16[256,512]{0,1:T(8,128)(2,1)S(1)} %get-tuple-element.412), channel_id=1, source_target_pairs={{0,1},{1,2},{2,3},{3,4},{4,5},{5,6},{6,7},{7,8},{8,9},{9,10},{10,1... | collective-permute-start | bytes 786440 | tf_op jit(solution)/shard_map/while/body/eval_jaxpr/ppermute | solution.py:57
  451.1 12.8 %collective-permute-start.1 = (bf16[256,512]{0,1:T(8,128)(2,1)S(1)}, bf16[256,512]{0,1:T(8,128)(2,1)S(1)}, u32[]{:S(2)}, u32[]{:S(2)}) collective-permute-start(bf16[256,512]{0,1:T(8,128)(2,1)S(1)} %get-tuple-element.413), channel_id=1, source_target_pairs={{0,1},{1,2},{2,3},{3,4},{4,5},{5,6},{6,7},{7,8},{8,9},{9,10},{10,1... | collective-permute-start | bytes 786440 | tf_op jit(solution)/shard_map/while/body/eval_jaxpr/ppermute | solution.py:57
  (19 other events, 28.8 us)
where the time goes:
time: 475 us; the launch traced here: 472 us
  waiting for transfers between devices  139 us (29%)
  between operations  117 us (25%)
  starting transfers between devices  62.4 us (13%)
  matrix products  51 us (11%)
  local copies, waits for them, and re-layouts  40 us (8%)
  blocking collectives  35 us (7%)
  other arithmetic  26.6 us (6%)
    ppermute x32, waiting for transfers between devices, from_behind(): return lax.ppermute(array, axis, pairs)  139 us
    ppermute x32, starting transfers between devices, from_behind(): return lax.ppermute(array, axis, pairs)  62.4 us
    dot_general x17, matrix products, attend(): jnp.einsum('kgtl,lkd->tkgd', weights, v_heads, preferred_element_type=jnp...  36 us
    unnamed x4, blocking collectives  35 us
    while x112, local copies, waits for them, and re-layouts  21 us
    reduce_sum x17, other arithmetic, attend(): total_new = total * factor + jnp.sum(expo, axis=-1)  17.6 us
    dot_general x17, matrix products, attend(): jnp.einsum('tkgd,lkd->kgtl', q_heads, k_heads, preferred_element_type=jnp...  15 us
  transfers between devices with their start and end apart: 32, of which 32 were waited for; matrix products, arithmetic and copies ran while one was open for 7% of the time, Pallas kernels for 0%

commit v1 on v0

v1 whole, which is shorter than its diff:
```python
import math

import jax
import jax.numpy as jnp
from jax import lax
from jax.experimental import pallas as pl
from jax.experimental.pallas import tpu as pltpu
from jax.sharding import Mesh
from jax.sharding import PartitionSpec as P

Q_HEADS = 16
KV_HEADS = 4
GROUP = Q_HEADS // KV_HEADS
HEAD_DIM = 128
WINDOW = 4096
TOK = 256
GRP_SEQ = ("grp", "seq_0", "seq_1", "seq_2")
NX, NZ = 4, 8
CHIPS = 128
REACH = WINDOW // (2 * TOK)
SLOTS = 2 * REACH + 1
FWD = 3
ONES = 16
NEG = -1e30
SCALE = 1.0 / math.sqrt(HEAD_DIM)
LOG2 = SCALE * math.log2(math.e)
MESH = pl.DeviceIdType.MESH


def kernel(q_hbm, k_hbm, v_hbm, seg_hbm, out_ref, lse_ref, kv, seg, qv, qt, acc, top, load_sem, recv_sem, send_sem, seg_recv, seg_send):
    y, x, z, core = (lax.axis_index(a) for a in GRP_SEQ)
    chip = (y * NX + x) * NZ + z

    def at(c, k):
        c = lax.rem(c + CHIPS, CHIPS)
        return (c // (NX * NZ), lax.rem(c // NZ, NX), lax.rem(c, NZ), k)

    ahead, behind = at(chip + 1, core), at(chip - 1, core)
    far, near = at(chip + REACH, core), at(chip - REACH, core)
    other = at(chip, 1 - core)

    loads = []
    for g in range(KV_HEADS):
        cols = pl.ds(g * HEAD_DIM, HEAD_DIM)
        loads.append(pltpu.make_async_copy(k_hbm.at[:, cols], kv.at[0, g, 0], load_sem.at[2 * g]))
        loads.append(pltpu.make_async_copy(v_hbm.at[:, cols], kv.at[0, g, 1], load_sem.at[2 * g + 1]))
    load_seg = pltpu.make_async_copy(seg_hbm, seg.at[0], load_sem.at[2 * KV_HEADS])
    load_q = pltpu.make_async_copy(q_hbm, qv, load_sem.at[2 * KV_HEADS + 1])
    load_seg.start()
    for copy in loads:
        copy.start()
    load_q.start()

    barrier = pltpu.get_barrier_semaphore()
    for peer in (ahead, behind, far, near, other):
        pl.semaphore_signal(barrier, inc=1, device_id=peer, device_id_type=MESH)
    pl.semaphore_wait(barrier, 5)

    def moved(src, g, dst, row, peer):
        return pltpu.make_async_remote_copy(
            src_ref=kv.at[src, g], dst_ref=kv.at[dst, g], send_sem=send_sem.at[row, g],
            recv_sem=recv_sem.at[dst, g], device_id=peer, device_id_type=MESH)

    def moved_seg(src, dst, row, peer):
        return pltpu.make_async_remote_copy(
            src_ref=seg.at[src], dst_ref=seg.at[dst], send_sem=seg_send.at[row],
            recv_sem=seg_recv.at[dst], device_id=peer, device_id_type=MESH)

    def send(src, g, dst, row, peer):
        @pl.when(g == 0)
        def _():
            moved_seg(src, dst, row, peer).start()

        moved(src, g, dst, row, peer).start()

    def arrive(slot, g):
        @pl.when(g == 0)
        def _():
            moved_seg(slot, slot, 0, other).wait_recv()

        moved(slot, g, slot, 0, other).wait_recv()

    def share(j, g):
        t = j - core
        send(j, g, REACH + 1 + t, 8 + t, other)

    load_seg.wait()
    for g in range(KV_HEADS):
        loads[2 * g].wait()
        loads[2 * g + 1].wait()
        send(0, g, REACH, 7, far)
        send(0, g, 1, 0, ahead)

        @pl.when(core == 0)
        def _():
            share(0, g)

    load_q.wait()

    def turn(h, carry):
        qt[h] = qv[:, pl.ds(pl.multiple_of(h * HEAD_DIM, HEAD_DIM), HEAD_DIM)].T
        return carry

    lax.fori_loop(0, Q_HEADS, turn, 0)

    mine = seg[0]
    mine_col = jnp.broadcast_to(mine.astype(jnp.float32), (HEAD_DIM, TOK)).T
    key_pos = lax.broadcasted_iota(jnp.int32, (TOK, TOK), 0)
    q_pos = lax.broadcasted_iota(jnp.int32, (TOK, TOK), 1)
    mine_col = jnp.concatenate([mine_col, mine_col], axis=1)
    diagonal = (mine_col == jnp.broadcast_to(mine.astype(jnp.float32), (TOK, TOK))) & (key_pos <= q_pos)
    q_row = lax.broadcasted_iota(jnp.int32, (1, TOK), 1)
    q_first = mine == mine[:, :1]

    def values_of(slot, g):
        ones = jnp.ones((ONES, TOK), jnp.bfloat16)
        return jnp.concatenate([kv[slot, g, 1].T, ones], axis=0)

    def scores_of(keys, h):
        return jnp.dot(keys, qt[h], preferred_element_type=jnp.float32)

    def own_block(g, carry):
        keys, values = kv[0, g, 0], values_of(0, g)
        for i in range(GROUP):
            h = g * GROUP + i
            s = jnp.where(diagonal, scores_of(keys, h), NEG)
            m = jnp.max(s, axis=0, keepdims=True)
            p = jnp.exp2(s * LOG2 - m * LOG2).astype(jnp.bfloat16)
            acc[h] = jnp.dot(values, p, preferred_element_type=jnp.float32)
            top[h] = m
        return carry

    lax.fori_loop(0, KV_HEADS, own_block, 0)

    def attend(slot, g):
        back = jnp.where(slot <= REACH, 2 * slot, 2 * (slot - REACH) - 1)
        before = jnp.sum(jnp.where(seg[slot] < mine[:, :1], 1.0, 0.0), axis=1, keepdims=True).astype(jnp.int32)
        lower = jnp.where(q_first, jnp.broadcast_to(before, (1, TOK)), TOK)
        lower = jnp.maximum(lower, jnp.where(back == 2 * REACH, q_row + 1, 0))
        lower = jnp.maximum(lower, jnp.where(2 * chip + core < back, TOK, 0))
        allowed = key_pos >= lower
        keys, values = kv[slot, g, 0], values_of(slot, g)
        for i in range(GROUP):
            h = g * GROUP + i
            s = jnp.where(allowed, scores_of(keys, h), NEG)
            old = top[h]
            m = jnp.maximum(old, jnp.max(s, axis=0, keepdims=True))
            p = jnp.exp2(s * LOG2 - m * LOG2).astype(jnp.bfloat16)
            update = jnp.dot(values, p, preferred_element_type=jnp.float32)
            acc[h] = acc[h] * jnp.exp2((old - m) * LOG2) + update
            top[h] = m

    def tick(t, carry):
        @pl.when(t < KV_HEADS)
        def _():
            arrive(REACH, t)
            send(REACH, t, REACH - 1, 3, behind)

            @pl.when(core == 1)
            def _():
                share(REACH, t)

        @pl.when(t < FWD * KV_HEADS)
        def _():
            j, g = 1 + t // KV_HEADS, lax.rem(t, KV_HEADS)
            arrive(j, g)

            @pl.when(j < FWD)
            def _():
                send(j, g, j + 1, j, ahead)

            share(j, g)

        @pl.when((t >= 1) & (t <= (REACH - 1 - FWD) * KV_HEADS))
        def _():
            b = t - 1
            j, g = REACH - 1 - b // KV_HEADS, lax.rem(b, KV_HEADS)
            arrive(j, g)

            @pl.when(j > FWD + 1)
            def _():
                send(j, g, j - 1, 3 + REACH - j, behind)

            share(j, g)

        def source(r, carry):
            late = lax.rem(r, 2)
            u = t - late
            kind = r // 2
            b = u - jnp.where(kind == 1, 1, 0)
            steps = jnp.where(kind == 0, FWD, jnp.where(kind == 1, REACH - 1 - FWD, 1)) * KV_HEADS
            valid = (b >= 0) & (b < steps)
            bb = jnp.maximum(b, 0)
            j = jnp.where(kind == 0, 1 + bb // KV_HEADS, jnp.where(kind == 1, REACH - 1 - bb // KV_HEADS, REACH))
            g = lax.rem(bb, KV_HEADS)
            paired = jnp.where(kind == 2, 2 * REACH - (REACH - 1) * core, REACH + j + core)
            slot = jnp.where(late == 1, paired, j)

            @pl.when(valid)
            def _():
                @pl.when(late == 1)
                def _():
                    arrive(slot, g)

                attend(slot, g)

            return carry

        lax.fori_loop(0, 6, source, 0)
        return carry

    lax.fori_loop(0, (REACH - 1 - FWD) * KV_HEADS + 2, tick, 0)

    def finish(h, carry):
        total = acc[h, HEAD_DIM:HEAD_DIM + 1, :]
        part = acc[h, :HEAD_DIM, :] / total
        out_ref[:, pl.ds(pl.multiple_of(h * HEAD_DIM, HEAD_DIM), HEAD_DIM)] = part.T.astype(jnp.bfloat16)
        lse_ref[pl.ds(h, 1), :] = top[h] * SCALE + jnp.log(total)
        return carry

    lax.fori_loop(0, Q_HEADS, finish, 0)

    def drain(i, carry):
        row = i // KV_HEADS
        g = lax.rem(i, KV_HEADS)
        moved(0, g, 1, row, other).wait_send()

        @pl.when(g == 0)
        def _():
            moved_seg(0, 1, row, other).wait_send()

        return carry

    lax.fori_loop(0, 16 * KV_HEADS, drain, 0)


def on_device(queries, key_rows, value_rows, segments):
    return pl.pallas_call(
        kernel,
        out_shape=(
            jax.ShapeDtypeStruct((TOK, Q_HEADS * HEAD_DIM), jnp.bfloat16),
            jax.ShapeDtypeStruct((Q_HEADS, TOK), jnp.float32),
        ),
        in_specs=[pl.BlockSpec(memory_space=pl.ANY)] * 4,
        out_specs=(pl.BlockSpec(memory_space=pltpu.VMEM), pl.BlockSpec(memory_space=pltpu.VMEM)),
        scratch_shapes=[
            pltpu.VMEM((SLOTS, KV_HEADS, 2, TOK, HEAD_DIM), jnp.bfloat16),
            pltpu.VMEM((SLOTS, 1, TOK), jnp.int32),
            pltpu.VMEM((TOK, Q_HEADS * HEAD_DIM), jnp.bfloat16),
            pltpu.VMEM((Q_HEADS, HEAD_DIM, TOK), jnp.bfloat16),
            pltpu.VMEM((Q_HEADS, HEAD_DIM + ONES, TOK), jnp.float32),
            pltpu.VMEM((Q_HEADS, 1, TOK), jnp.float32),
            pltpu.SemaphoreType.DMA((2 * KV_HEADS + 2,)),
            pltpu.SemaphoreType.DMA((SLOTS, KV_HEADS)),
            pltpu.SemaphoreType.DMA((16, KV_HEADS)),
            pltpu.SemaphoreType.DMA((SLOTS,)),
            pltpu.SemaphoreType.DMA((16,)),
        ],
        compiler_params=pltpu.CompilerParams(
            collective_id=0, has_side_effects=True, vmem_limit_bytes=60 * 1024 * 1024),
    )(queries, key_rows, value_rows, segments.reshape(1, TOK))


def solution(mesh):
    split = Mesh(mesh.devices.reshape(mesh.shape["grp"], NX, NZ, 2), GRP_SEQ)
    rows = P(GRP_SEQ, None)
    return jax.shard_map(
        on_device,
        mesh=split,
        in_specs=(rows, rows, rows, P(GRP_SEQ)),
        out_specs=(rows, P(None, GRP_SEQ)),
        check_vma=False,
    )
```

time: 475 us -> 129 us (0.27)
  the two profiles are of different devices: /device:TPU:8 before, /device:TPU:1 now
where the time goes in v1:
time: 129 us; the launch traced here: 128 us
  Pallas kernels  125 us (97%)
  local copies, waits for them, and re-layouts  2.92 us (2%)
    pallas_call x1, Pallas kernels, on_device(): pl.pallas_call(kernel, out_shape=(jax.ShapeDtypeStruct((TOK, Q_HEADS * HE...  125 us
    unnamed x4, local copies, waits for them, and re-layouts  2.92 us

profile of v1, /device:TPU:1, one launch (start us, length us, event | category | flops | bytes accessed | tf_op | source)
XLA Modules:
  0.0 128.5 jit_solution(9738754036916271546)
XLA Ops:
  0.6 124.9 %shard_map.59 = (bf16[256,2048]{1,0:T(8,128)(2,1)}, f32[16,256]{1,0:T(8,128)}) custom-call(bf16[256,2048]{1,0:T(8,128)(2,1)} %q_hbm.1, bf16[256,512]{1,0:T(8,128)(2,1)} %k_hbm.1, bf16[256,512]{1,0:T(8,128)(2,1)} %v_hbm.1, s32[1,256]{1,0:T(1,128)} %bitcast.1), custom_call_target="tpu_custom_call" | custom-call | tf_op jit(solution)/shard_map/pallas_call | solution.py:238
  125.5 0.0 copy-start
  125.6 2.3 %copy.8 = bf16[256,2048]{1,0:T(8,128)(2,1)} copy(bf16[256,2048]{1,0:T(8,128)(2,1)} %get-tuple-element.4) | data formatting | bytes 2097152
  127.9 0.0 copy-done
  127.9 0.6 copy.9
Async XLA Ops:
  125.5 2.3 %copy-start = (f32[16,256]{1,0:T(8,128)S(1)}, f32[16,256]{1,0:T(8,128)}, u32[]{:S(2)}) copy-start(f32[16,256]{1,0:T(8,128)} %get-tuple-element.5) | copy-start | bytes 49156

commit v2 on v1

--- a/solution.py
+++ b/solution.py
@@ -20,8 +20,10 @@
 REACH = WINDOW // (2 * TOK)
 SLOTS = 2 * REACH + 1
 FWD = 3
+BACK = REACH - 1 - FWD
 ONES = 16
 NEG = -1e30
+BIG = -(2.0**100)
 SCALE = 1.0 / math.sqrt(HEAD_DIM)
 LOG2 = SCALE * math.log2(math.e)
 MESH = pl.DeviceIdType.MESH
@@ -89,7 +91,10 @@
         loads[2 * g].wait()
         loads[2 * g + 1].wait()
         send(0, g, REACH, 7, far)
-        send(0, g, 1, 0, ahead)
+
+        @pl.when(z != NZ - 1)
+        def _():
+            send(0, g, 1, 0, ahead)
 
         @pl.when(core == 0)
         def _():
@@ -97,58 +102,73 @@
 
     load_q.wait()
 
+    mine = seg[0]
+    q_row = lax.broadcasted_iota(jnp.int32, (1, TOK), 1)
+    q_first = mine == mine[:, :1]
+    sub = lax.broadcasted_iota(jnp.int32, (HEAD_DIM, TOK), 0)
+    marks = jnp.where(sub == 0, 1.0, jnp.where(sub == 1, jnp.where(q_first, 0.0, 1.0), 0.0)).astype(jnp.bfloat16)
+
     def turn(h, carry):
-        qt[h] = qv[:, pl.ds(pl.multiple_of(h * HEAD_DIM, HEAD_DIM), HEAD_DIM)].T
+        g, i = h // GROUP, lax.rem(h, GROUP)
+        qt[g, i, :HEAD_DIM] = qv[:, pl.ds(pl.multiple_of(h * HEAD_DIM, HEAD_DIM), HEAD_DIM)].T
+        qt[g, i, HEAD_DIM:] = marks
         return carry
 
-    lax.fori_loop(0, Q_HEADS, turn, 0)
-
-    mine = seg[0]
     mine_col = jnp.broadcast_to(mine.astype(jnp.float32), (HEAD_DIM, TOK)).T
     key_pos = lax.broadcasted_iota(jnp.int32, (TOK, TOK), 0)
     q_pos = lax.broadcasted_iota(jnp.int32, (TOK, TOK), 1)
     mine_col = jnp.concatenate([mine_col, mine_col], axis=1)
     diagonal = (mine_col == jnp.broadcast_to(mine.astype(jnp.float32), (TOK, TOK))) & (key_pos <= q_pos)
-    q_row = lax.broadcasted_iota(jnp.int32, (1, TOK), 1)
-    q_first = mine == mine[:, :1]
+    lane = lax.broadcasted_iota(jnp.int32, (TOK, HEAD_DIM), 1)
+    key_row = lax.broadcasted_iota(jnp.int32, (TOK, HEAD_DIM), 0)
 
     def values_of(slot, g):
         ones = jnp.ones((ONES, TOK), jnp.bfloat16)
         return jnp.concatenate([kv[slot, g, 1].T, ones], axis=0)
 
-    def scores_of(keys, h):
-        return jnp.dot(keys, qt[h], preferred_element_type=jnp.float32)
-
-    def own_block(g, carry):
-        keys, values = kv[0, g, 0], values_of(0, g)
+    def heads(slot, g, keys, query_rows, mask, fresh):
+        values = values_of(slot, g)
+        old = None if fresh else [top[g, i] for i in range(GROUP)]
+
+        def scores_of(i):
+            return jnp.dot(keys, qt[g, i, :query_rows], preferred_element_type=jnp.float32)
+
+        after = scores_of(0)
+        maxima, factors, updates = [], [], []
         for i in range(GROUP):
-            h = g * GROUP + i
-            s = jnp.where(diagonal, scores_of(keys, h), NEG)
+            s = after
+            if i + 1 < GROUP:
+                after = scores_of(i + 1)
+            if mask is not None:
+                s = jnp.where(mask(), s, NEG)
             m = jnp.max(s, axis=0, keepdims=True)
+            if not fresh:
+                m = jnp.maximum(old[i], m)
+                factors.append(jnp.exp2((old[i] - m) * LOG2))
             p = jnp.exp2(s * LOG2 - m * LOG2).astype(jnp.bfloat16)
-            acc[h] = jnp.dot(values, p, preferred_element_type=jnp.float32)
-            top[h] = m
-        return carry
-
-    lax.fori_loop(0, KV_HEADS, own_block, 0)
-
-    def attend(slot, g):
+            update = jnp.dot(values, p, preferred_element_type=jnp.float32)
+            if fresh:
+                acc[g, i] = update
+            else:
+                acc[g, i] = acc[g, i] * factors[i] + update
+            maxima.append(m)
+        for i in range(GROUP):
+            top[g, i] = maxima[i]
+
+    def attend(slot, g, window):
         back = jnp.where(slot <= REACH, 2 * slot, 2 * (slot - REACH) - 1)
         before = jnp.sum(jnp.where(seg[slot] < mine[:, :1], 1.0, 0.0), axis=1, keepdims=True).astype(jnp.int32)
-        lower = jnp.where(q_first, jnp.broadcast_to(before, (1, TOK)), TOK)
-        lower = jnp.maximum(lower, jnp.where(back == 2 * REACH, q_row + 1, 0))
-        lower = jnp.maximum(lower, jnp.where(2 * chip + core < back, TOK, 0))
-        allowed = key_pos >= lower
-        keys, values = kv[slot, g, 0], values_of(slot, g)
-        for i in range(GROUP):
-            h = g * GROUP + i
-            s = jnp.where(allowed, scores_of(keys, h), NEG)
-            old = top[h]
-            m = jnp.maximum(old, jnp.max(s, axis=0, keepdims=True))
-            p = jnp.exp2(s * LOG2 - m * LOG2).astype(jnp.bfloat16)
-            update = jnp.dot(values, p, preferred_element_type=jnp.float32)
-            acc[h] = acc[h] * jnp.exp2((old - m) * LOG2) + update
-            top[h] = m
+        before = jnp.maximum(before, jnp.where(2 * chip + core < back, TOK, 0))
+        if window:
+            lower = jnp.where(q_first, jnp.broadcast_to(before, (1, TOK)), TOK)
+            lower = jnp.maximum(lower, q_row + 1)
+            heads(slot, g, kv[slot, g, 0], HEAD_DIM, lambda: key_pos >= lower, False)
+        else:
+            closed = jnp.where(key_row < before, BIG, 0.0)
+            marks = jnp.where(lane == 0, closed, jnp.where(lane == 1, BIG, 0.0)).astype(jnp.bfloat16)
+            heads(slot, g, jnp.concatenate([kv[slot, g, 0], marks], axis=1), 2 * HEAD_DIM, None, False)
+
+    lag = jnp.where(z == 0, 5, jnp.where(z == 1, 3, 2))
 
     def tick(t, carry):
         @pl.when(t < KV_HEADS)
@@ -160,9 +180,29 @@
             def _():
                 share(REACH, t)
 
-        @pl.when(t < FWD * KV_HEADS)
-        def _():
-            j, g = 1 + t // KV_HEADS, lax.rem(t, KV_HEADS)
+        @pl.when((t == KV_HEADS - 1) & (z == NZ - 1))
+        def _():
+            for g in range(KV_HEADS):
+                send(0, g, 1, 0, ahead)
+
+        b = t - 1
+
+        @pl.when((b >= 0) & (b < BACK * KV_HEADS))
+        def _():
+            j, g = REACH - 1 - b // KV_HEADS, lax.rem(b, KV_HEADS)
+            arrive(j, g)
+
+            @pl.when(j > FWD + 1)
+            def _():
+                send(j, g, j - 1, 3 + REACH - j, behind)
+
+            share(j, g)
+
+        f = t - lag
+
+        @pl.when((f >= 0) & (f < FWD * KV_HEADS))
+        def _():
+            j, g = 1 + f // KV_HEADS, lax.rem(f, KV_HEADS)
             arrive(j, g)
 
             @pl.when(j < FWD)
@@ -171,51 +211,47 @@
 
             share(j, g)
 
-        @pl.when((t >= 1) & (t <= (REACH - 1 - FWD) * KV_HEADS))
-        def _():
-            b = t - 1
-            j, g = REACH - 1 - b // KV_HEADS, lax.rem(b, KV_HEADS)
-            arrive(j, g)
-
-            @pl.when(j > FWD + 1)
-            def _():
-                send(j, g, j - 1, 3 + REACH - j, behind)
-
-            share(j, g)
+        @pl.when(t < KV_HEADS)
+        def _():
+            lax.fori_loop(t * GROUP, (t + 1) * GROUP, turn, 0)
+            heads(0, t, kv[0, t, 0], HEAD_DIM, lambda: diagonal, True)
 
         def source(r, carry):
-            late = lax.rem(r, 2)
-            u = t - late
             kind = r // 2
-            b = u - jnp.where(kind == 1, 1, 0)
-            steps = jnp.where(kind == 0, FWD, jnp.where(kind == 1, REACH - 1 - FWD, 1)) * KV_HEADS
-            valid = (b >= 0) & (b < steps)
-            bb = jnp.maximum(b, 0)
-            j = jnp.where(kind == 0, 1 + bb // KV_HEADS, jnp.where(kind == 1, REACH - 1 - bb // KV_HEADS, REACH))
-            g = lax.rem(bb, KV_HEADS)
+            late = jnp.where(kind == 2, 1, lax.rem(r, 2))
+            u = t - late - jnp.where(kind == 0, lag, jnp.where(kind == 1, 1, KV_HEADS - 1))
+            steps = jnp.where(kind == 0, FWD, jnp.where(kind == 1, BACK, 1)) * KV_HEADS
+            v = jnp.maximum(u, 0)
+            j = jnp.where(kind == 0, 1 + v // KV_HEADS, REACH - 1 - v // KV_HEADS)
+            g = lax.rem(v, KV_HEADS)
             paired = jnp.where(kind == 2, 2 * REACH - (REACH - 1) * core, REACH + j + core)
             slot = jnp.where(late == 1, paired, j)
 
-            @pl.when(valid)
+            @pl.when((u >= 0) & (u < steps))
             def _():
                 @pl.when(late == 1)
                 def _():
                     arrive(slot, g)
 
-                attend(slot, g)
+                attend(slot, g, False)
 
             return carry
 
-        lax.fori_loop(0, 6, source, 0)
+        @pl.when((t >= KV_HEADS) & (t < 2 * KV_HEADS))
+        def _():
+            attend(REACH, t - KV_HEADS, True)
+
+        lax.fori_loop(0, 5, source, 0)
         return carry
 
-    lax.fori_loop(0, (REACH - 1 - FWD) * KV_HEADS + 2, tick, 0)
+    lax.fori_loop(0, BACK * KV_HEADS + 2, tick, 0)
 
     def finish(h, carry):
-        total = acc[h, HEAD_DIM:HEAD_DIM + 1, :]
-        part = acc[h, :HEAD_DIM, :] / total
+        g, i = h // GROUP, lax.rem(h, GROUP)
+        total = acc[g, i, HEAD_DIM:HEAD_DIM + 1, :]
+        part = acc[g, i, :HEAD_DIM, :] / total
         out_ref[:, pl.ds(pl.multiple_of(h * HEAD_DIM, HEAD_DIM), HEAD_DIM)] = part.T.astype(jnp.bfloat16)
-        lse_ref[pl.ds(h, 1), :] = top[h] * SCALE + jnp.log(total)
+        lse_ref[pl.ds(h, 1), :] = top[g, i] * SCALE + jnp.log(total)
         return carry
 
     lax.fori_loop(0, Q_HEADS, finish, 0)
@@ -247,9 +283,9 @@
             pltpu.VMEM((SLOTS, KV_HEADS, 2, TOK, HEAD_DIM), jnp.bfloat16),
             pltpu.VMEM((SLOTS, 1, TOK), jnp.int32),
             pltpu.VMEM((TOK, Q_HEADS * HEAD_DIM), jnp.bfloat16),
-            pltpu.VMEM((Q_HEADS, HEAD_DIM, TOK), jnp.bfloat16),
-            pltpu.VMEM((Q_HEADS, HEAD_DIM + ONES, TOK), jnp.float32),
-            pltpu.VMEM((Q_HEADS, 1, TOK), jnp.float32),
+            pltpu.VMEM((KV_HEADS, GROUP, 2 * HEAD_DIM, TOK), jnp.bfloat16),
+            pltpu.VMEM((KV_HEADS, GROUP, HEAD_DIM + ONES, TOK), jnp.float32),
+            pltpu.VMEM((KV_HEADS, GROUP, 1, TOK), jnp.float32),
             pltpu.SemaphoreType.DMA((2 * KV_HEADS + 2,)),
             pltpu.SemaphoreType.DMA((SLOTS, KV_HEADS)),
             pltpu.SemaphoreType.DMA((16, KV_HEADS)),

time: 129 us -> 87.5 us (0.68)
  Pallas kernels: 125 us -> 83.8 us
    pallas_call x1, Pallas kernels: 125 us -> 83.8 us  [on_device(): pl.pallas_call(kernel, out_shape=(jax.ShapeDtypeStruct((TOK, Q_HEADS * HE...]
where the time goes in v2:
time: 87.5 us; the launch traced here: 87.4 us
  Pallas kernels  83.8 us (96%)
  local copies, waits for them, and re-layouts  2.92 us (3%)
    pallas_call x1, Pallas kernels, on_device(): pl.pallas_call(kernel, out_shape=(jax.ShapeDtypeStruct((TOK, Q_HEADS * HE...  83.8 us
    unnamed x4, local copies, waits for them, and re-layouts  2.92 us

profile of v2, /device:TPU:1, one launch (start us, length us, event | category | flops | bytes accessed | tf_op | source)
XLA Modules:
  0.0 87.4 jit_solution(12786634404168073291)
XLA Ops:
  0.6 83.8 %shard_map.59 = (bf16[256,2048]{1,0:T(8,128)(2,1)}, f32[16,256]{1,0:T(8,128)}) custom-call(bf16[256,2048]{1,0:T(8,128)(2,1)} %q_hbm.1, bf16[256,512]{1,0:T(8,128)(2,1)} %k_hbm.1, bf16[256,512]{1,0:T(8,128)(2,1)} %v_hbm.1, s32[1,256]{1,0:T(1,128)} %bitcast.1), custom_call_target="tpu_custom_call" | custom-call | tf_op jit(solution)/shard_map/pallas_call | solution.py:274
  84.4 0.0 copy-start
  84.5 2.3 %copy.8 = bf16[256,2048]{1,0:T(8,128)(2,1)} copy(bf16[256,2048]{1,0:T(8,128)(2,1)} %get-tuple-element.4) | data formatting | bytes 2097152
  86.8 0.0 copy-done
  86.8 0.6 copy.9
Async XLA Ops:
  84.4 2.3 %copy-start = (f32[16,256]{1,0:T(8,128)S(1)}, f32[16,256]{1,0:T(8,128)}, u32[]{:S(2)}) copy-start(f32[16,256]{1,0:T(8,128)} %get-tuple-element.5) | copy-start | bytes 49156

commit v3 on v2

--- a/solution.py
+++ b/solution.py
@@ -29,7 +29,7 @@
 MESH = pl.DeviceIdType.MESH
 
 
-def kernel(q_hbm, k_hbm, v_hbm, seg_hbm, out_ref, lse_ref, kv, seg, qv, qt, acc, top, load_sem, recv_sem, send_sem, seg_recv, seg_send):
+def kernel(q_hbm, k_hbm, v_hbm, seg_hbm, out_ref, lse_ref, kv, seg, qv, qt, acc, top, bias, score, load_sem, recv_sem, send_sem, seg_recv, seg_send):
     y, x, z, core = (lax.axis_index(a) for a in GRP_SEQ)
     chip = (y * NX + x) * NZ + z
 
@@ -115,58 +115,71 @@
         return carry
 
     mine_col = jnp.broadcast_to(mine.astype(jnp.float32), (HEAD_DIM, TOK)).T
+    mine_col = jnp.concatenate([mine_col, mine_col], axis=1)
     key_pos = lax.broadcasted_iota(jnp.int32, (TOK, TOK), 0)
     q_pos = lax.broadcasted_iota(jnp.int32, (TOK, TOK), 1)
-    mine_col = jnp.concatenate([mine_col, mine_col], axis=1)
-    diagonal = (mine_col == jnp.broadcast_to(mine.astype(jnp.float32), (TOK, TOK))) & (key_pos <= q_pos)
+    same = mine_col == jnp.broadcast_to(mine.astype(jnp.float32), (TOK, TOK))
+    bias[...] = jnp.where(same & (key_pos <= q_pos), 0.0, NEG)
     lane = lax.broadcasted_iota(jnp.int32, (TOK, HEAD_DIM), 1)
     key_row = lax.broadcasted_iota(jnp.int32, (TOK, HEAD_DIM), 0)
 
-    def values_of(slot, g):
-        ones = jnp.ones((ONES, TOK), jnp.bfloat16)
-        return jnp.concatenate([kv[slot, g, 1].T, ones], axis=0)
-
-    def heads(slot, g, keys, query_rows, mask, fresh):
-        values = values_of(slot, g)
-        old = None if fresh else [top[g, i] for i in range(GROUP)]
-
-        def scores_of(i):
-            return jnp.dot(keys, qt[g, i, :query_rows], preferred_element_type=jnp.float32)
-
-        after = scores_of(0)
-        maxima, factors, updates = [], [], []
-        for i in range(GROUP):
-            s = after
-            if i + 1 < GROUP:
-                after = scores_of(i + 1)
-            if mask is not None:
-                s = jnp.where(mask(), s, NEG)
-            m = jnp.max(s, axis=0, keepdims=True)
-            if not fresh:
-                m = jnp.maximum(old[i], m)
-                factors.append(jnp.exp2((old[i] - m) * LOG2))
-            p = jnp.exp2(s * LOG2 - m * LOG2).astype(jnp.bfloat16)
-            update = jnp.dot(values, p, preferred_element_type=jnp.float32)
-            if fresh:
-                acc[g, i] = update
-            else:
-                acc[g, i] = acc[g, i] * factors[i] + update
-            maxima.append(m)
-        for i in range(GROUP):
-            top[g, i] = maxima[i]
-
-    def attend(slot, g, window):
+    def keys_of(slot, g):
         back = jnp.where(slot <= REACH, 2 * slot, 2 * (slot - REACH) - 1)
         before = jnp.sum(jnp.where(seg[slot] < mine[:, :1], 1.0, 0.0), axis=1, keepdims=True).astype(jnp.int32)
         before = jnp.maximum(before, jnp.where(2 * chip + core < back, TOK, 0))
-        if window:
-            lower = jnp.where(q_first, jnp.broadcast_to(before, (1, TOK)), TOK)
-            lower = jnp.maximum(lower, q_row + 1)
-            heads(slot, g, kv[slot, g, 0], HEAD_DIM, lambda: key_pos >= lower, False)
-        else:
-            closed = jnp.where(key_row < before, BIG, 0.0)
-            marks = jnp.where(lane == 0, closed, jnp.where(lane == 1, BIG, 0.0)).astype(jnp.bfloat16)
-            heads(slot, g, jnp.concatenate([kv[slot, g, 0], marks], axis=1), 2 * HEAD_DIM, None, False)
+        closed = jnp.where(key_row < before, BIG, 0.0)
+        columns = jnp.where(lane == 0, closed, jnp.where(lane == 1, BIG, 0.0)).astype(jnp.bfloat16)
+        return jnp.concatenate([kv[slot, g, 0], columns], axis=1)
+
+    def values_of(slots, g):
+        values = jnp.concatenate([kv[slot, g, 1].T for slot in slots], axis=1)
+        return jnp.concatenate([values, jnp.ones((ONES, TOK * len(slots)), jnp.bfloat16)], axis=0)
+
+    def first_blocks(g):
+        own, old, values = kv[0, g, 0], keys_of(REACH, g), values_of((0, REACH), g)
+
+        causal = key_pos <= q_pos
+
+        def scores_of(i):
+            s_own = jnp.dot(own, qt[g, i, :HEAD_DIM], preferred_element_type=jnp.float32)
+            s_old = jnp.dot(old, qt[g, i], preferred_element_type=jnp.float32)
+            s = jnp.where(causal, s_own + bias[...], s_old)
+            score[i, :TOK] = s
+            return jnp.max(s, axis=0, keepdims=True)
+
+        maxima = [scores_of(0)]
+        for i in range(GROUP):
+            if i + 1 < GROUP:
+                maxima.append(scores_of(i + 1))
+            m = maxima[i]
+            p = jnp.exp2(score[i, :TOK] * LOG2 - m * LOG2)
+            p = jnp.concatenate([jnp.where(causal, p, 0.0), jnp.where(causal, 0.0, p)], axis=0).astype(jnp.bfloat16)
+            acc[g, i] = jnp.dot(values, p, preferred_element_type=jnp.float32)
+        for i in range(GROUP):
+            top[g, i] = maxima[i]
+
+    def attend(slots, g):
+        keys = jnp.concatenate([keys_of(slot, g) for slot in slots], axis=0)
+        values = values_of(slots, g)
+        old = [top[g, i] for i in range(GROUP)]
+
+        length = TOK * len(slots)
+
+        def scores_of(i):
+            s = jnp.dot(keys, qt[g, i], preferred_element_type=jnp.float32)
+            score[i, :length] = s
+            return jnp.maximum(old[i], jnp.max(s, axis=0, keepdims=True))
+
+        maxima = [scores_of(0)]
+        for i in range(GROUP):
+            if i + 1 < GROUP:
+                maxima.append(scores_of(i + 1))
+            m = maxima[i]
+            w = jnp.exp2(score[i, :length] * LOG2 - m * LOG2).astype(jnp.bfloat16)
+            update = jnp.dot(values, w, preferred_element_type=jnp.float32)
+            acc[g, i] = acc[g, i] * jnp.exp2((old[i] - m) * LOG2) + update
+        for i in range(GROUP):
+            top[g, i] = maxima[i]
 
     lag = jnp.where(z == 0, 5, jnp.where(z == 1, 3, 2))
 
@@ -214,34 +227,28 @@
         @pl.when(t < KV_HEADS)
         def _():
             lax.fori_loop(t * GROUP, (t + 1) * GROUP, turn, 0)
-            heads(0, t, kv[0, t, 0], HEAD_DIM, lambda: diagonal, True)
+            first_blocks(t)
 
         def source(r, carry):
-            kind = r // 2
-            late = jnp.where(kind == 2, 1, lax.rem(r, 2))
-            u = t - late - jnp.where(kind == 0, lag, jnp.where(kind == 1, 1, KV_HEADS - 1))
-            steps = jnp.where(kind == 0, FWD, jnp.where(kind == 1, BACK, 1)) * KV_HEADS
+            u = t - jnp.where(r == 0, 2, lag + 1)
             v = jnp.maximum(u, 0)
-            j = jnp.where(kind == 0, 1 + v // KV_HEADS, REACH - 1 - v // KV_HEADS)
+            j = jnp.where(r == 0, REACH - 1 - v // KV_HEADS, 1 + v // KV_HEADS)
             g = lax.rem(v, KV_HEADS)
-            paired = jnp.where(kind == 2, 2 * REACH - (REACH - 1) * core, REACH + j + core)
-            slot = jnp.where(late == 1, paired, j)
-
-            @pl.when((u >= 0) & (u < steps))
+
+            @pl.when((u >= 0) & (u < jnp.where(r == 0, BACK, FWD) * KV_HEADS))
             def _():
-                @pl.when(late == 1)
-                def _():
-                    arrive(slot, g)
-
-                attend(slot, g, False)
+                arrive(REACH + j + core, g)
+                attend((j, REACH + j + core), g)
 
             return carry
 
         @pl.when((t >= KV_HEADS) & (t < 2 * KV_HEADS))
         def _():
-            attend(REACH, t - KV_HEADS, True)
-
-        lax.fori_loop(0, 5, source, 0)
+            slot = 2 * REACH - (REACH - 1) * core
+            arrive(slot, t - KV_HEADS)
+            attend((slot,), t - KV_HEADS)
+
+        lax.fori_loop(0, 2, source, 0)
         return carry
 
     lax.fori_loop(0, BACK * KV_HEADS + 2, tick, 0)
@@ -286,6 +293,8 @@
             pltpu.VMEM((KV_HEADS, GROUP, 2 * HEAD_DIM, TOK), jnp.bfloat16),
             pltpu.VMEM((KV_HEADS, GROUP, HEAD_DIM + ONES, TOK), jnp.float32),
             pltpu.VMEM((KV_HEADS, GROUP, 1, TOK), jnp.float32),
+            pltpu.VMEM((TOK, TOK), jnp.float32),
+            pltpu.VMEM((4, 2 * TOK, TOK), jnp.float32),
             pltpu.SemaphoreType.DMA((2 * KV_HEADS + 2,)),
             pltpu.SemaphoreType.DMA((SLOTS, KV_HEADS)),
             pltpu.SemaphoreType.DMA((16, KV_HEADS)),
@@ -293,8 +302,8 @@
             pltpu.SemaphoreType.DMA((16,)),
         ],
         compiler_params=pltpu.CompilerParams(
-            collective_id=0, has_side_effects=True, vmem_limit_bytes=60 * 1024 * 1024),
-    )(queries, key_rows, value_rows, segments.reshape(1, TOK))
+            collective_id=0, has_side_effects=True, vmem_limit_bytes=30 * 1024 * 1024),
+    )(*(pltpu.with_memory_space_constraint(a, pltpu.HBM) for a in (queries, key_rows, value_rows)), segments.reshape(1, TOK))
 
 
 def solution(mesh):

time: 87.5 us -> 75.5 us (0.86)
  Pallas kernels: 83.8 us -> 72.5 us
    pallas_call x1, Pallas kernels: 83.8 us -> 72.5 us  [on_device(): pl.pallas_call(kernel, out_shape=(jax.ShapeDtypeStruct((TOK, Q_HEADS * HE...]
where the time goes in v3:
time: 75.5 us; the launch traced here: 75.4 us
  Pallas kernels  72.5 us (96%)
  local copies, waits for them, and re-layouts  2.25 us (3%)
    pallas_call x1, Pallas kernels, on_device(): pl.pallas_call(kernel, out_shape=(jax.ShapeDtypeStruct((TOK, Q_HEADS * HE...  72.5 us
    unnamed x4, local copies, waits for them, and re-layouts  2.25 us

profile of v3, /device:TPU:1, one launch (start us, length us, event | category | flops | bytes accessed | tf_op | source)
XLA Modules:
  0.0 75.4 jit_solution(12462298988511211076)
XLA Ops:
  0.6 0.0 copy-start
  0.6 0.7 copy-done
  1.3 72.5 %shard_map.59 = (bf16[256,2048]{1,0:T(8,128)(2,1)S(1)}, f32[16,256]{1,0:T(8,128)S(1)}) custom-call(bf16[256,2048]{1,0:T(8,128)(2,1)} %q_hbm.1, bf16[256,512]{1,0:T(8,128)(2,1)} %k_hbm.1, bf16[256,512]{1,0:T(8,128)(2,1)} %v_hbm.1, s32[1,256]{1,0:T(1,128)S(1)} %bitcast.1), custom_call_target="tpu_custom_call" | custom-call | tf_op jit(solution)/shard_map/pallas_call | solution.py:281
  73.8 1.0 %copy.8 = bf16[256,2048]{1,0:T(8,128)(2,1)} copy(bf16[256,2048]{1,0:T(8,128)(2,1)S(1)} %get-tuple-element.4) | data formatting | bytes 2097152
  74.8 0.6 copy.9
Async XLA Ops:
  0.6 0.7 copy-start

commit v4 on v3

--- a/solution.py
+++ b/solution.py
@@ -41,6 +41,21 @@
     far, near = at(chip + REACH, core), at(chip - REACH, core)
     other = at(chip, 1 - core)
 
+    first, last = z == 0, z == NZ - 1
+
+    def real(c, j):
+        c = lax.rem(c + CHIPS, CHIPS)
+        return (c >= REACH) | (j <= c)
+
+    def live(c, j):
+        return real(c, j) | (j >= lax.rem(c + CHIPS, CHIPS) + REACH - 2)
+
+    def sent_ahead(j):
+        return ((j < FWD) | ((j == FWD) & (z == NZ - 2))) & live(chip, j) & live(chip + 1, j + 1)
+
+    def sent_behind(j):
+        return (j > FWD + 1) & live(chip, j) & live(chip - 1, j - 1) & jnp.logical_not(first & (j == FWD + 2))
+
     loads = []
     for g in range(KV_HEADS):
         cols = pl.ds(g * HEAD_DIM, HEAD_DIM)
@@ -84,15 +99,18 @@
 
     def share(j, g):
         t = j - core
-        send(j, g, REACH + 1 + t, 8 + t, other)
+        send(j, g, REACH + 1 + t, 9 + t, other)
 
     load_seg.wait()
     for g in range(KV_HEADS):
         loads[2 * g].wait()
         loads[2 * g + 1].wait()
-        send(0, g, REACH, 7, far)
-
-        @pl.when(z != NZ - 1)
+
+        @pl.when(live(chip + REACH, REACH))
+        def _():
+            send(0, g, REACH, 8, far)
+
+        @pl.when(sent_ahead(0) & jnp.logical_not(last))
         def _():
             send(0, g, 1, 0, ahead)
 
@@ -123,8 +141,7 @@
     lane = lax.broadcasted_iota(jnp.int32, (TOK, HEAD_DIM), 1)
     key_row = lax.broadcasted_iota(jnp.int32, (TOK, HEAD_DIM), 0)
 
-    def keys_of(slot, g):
-        back = jnp.where(slot <= REACH, 2 * slot, 2 * (slot - REACH) - 1)
+    def keys_of(slot, g, back):
         before = jnp.sum(jnp.where(seg[slot] < mine[:, :1], 1.0, 0.0), axis=1, keepdims=True).astype(jnp.int32)
         before = jnp.maximum(before, jnp.where(2 * chip + core < back, TOK, 0))
         closed = jnp.where(key_row < before, BIG, 0.0)
@@ -136,7 +153,8 @@
         return jnp.concatenate([values, jnp.ones((ONES, TOK * len(slots)), jnp.bfloat16)], axis=0)
 
     def first_blocks(g):
-        own, old, values = kv[0, g, 0], keys_of(REACH, g), values_of((0, REACH), g)
+        slot = jnp.where(real(chip, REACH), REACH, 0)
+        own, old, values = kv[0, g, 0], keys_of(slot, g, 2 * REACH), values_of((0, slot), g)
 
         causal = key_pos <= q_pos
 
@@ -159,7 +177,7 @@
             top[g, i] = maxima[i]
 
     def attend(slots, g):
-        keys = jnp.concatenate([keys_of(slot, g) for slot in slots], axis=0)
+        keys = jnp.concatenate([keys_of(slot, g, jnp.where(slot <= REACH, 2 * slot, 2 * (slot - REACH) - 1)) for slot in slots], axis=0)
         values = values_of(slots, g)
         old = [top[g, i] for i in range(GROUP)]
 
@@ -181,48 +199,62 @@
         for i in range(GROUP):
             top[g, i] = maxima[i]
 
-    lag = jnp.where(z == 0, 5, jnp.where(z == 1, 3, 2))
+    lag = jnp.where(first, 6, jnp.where(z == 1, 3, 1))
 
     def tick(t, carry):
-        @pl.when(t < KV_HEADS)
+        @pl.when((t < KV_HEADS) & live(chip, REACH))
         def _():
             arrive(REACH, t)
-            send(REACH, t, REACH - 1, 3, behind)
-
-            @pl.when(core == 1)
+
+            @pl.when(sent_behind(REACH))
+            def _():
+                send(REACH, t, REACH - 1, 4, behind)
+
+            @pl.when((core == 1) & real(chip, REACH))
             def _():
                 share(REACH, t)
 
-        @pl.when((t == KV_HEADS - 1) & (z == NZ - 1))
-        def _():
-            for g in range(KV_HEADS):
-                send(0, g, 1, 0, ahead)
-
         b = t - 1
-
-        @pl.when((b >= 0) & (b < BACK * KV_HEADS))
-        def _():
-            j, g = REACH - 1 - b // KV_HEADS, lax.rem(b, KV_HEADS)
-            arrive(j, g)
-
-            @pl.when(j > FWD + 1)
-            def _():
-                send(j, g, j - 1, 3 + REACH - j, behind)
-
-            share(j, g)
+        j_b, g_b = REACH - 1 - jnp.maximum(b, 0) // KV_HEADS, lax.rem(b + KV_HEADS, KV_HEADS)
+
+        @pl.when((b >= 0) & (b < BACK * KV_HEADS) & live(chip, j_b) & jnp.logical_not(last & (j_b == FWD + 1)))
+        def _():
+            arrive(j_b, g_b)
+
+            @pl.when(sent_behind(j_b))
+            def _():
+                send(j_b, g_b, j_b - 1, 4 + REACH - j_b, behind)
+
+            @pl.when(real(chip, j_b))
+            def _():
+                share(j_b, g_b)
+
+        k = t - 2
+
+        @pl.when((k >= 0) & (k < 2) & last & sent_ahead(0))
+        def _():
+            send(0, 2 * k, 1, 0, ahead)
+            send(0, 2 * k + 1, 1, 0, ahead)
+
+        r = t - 4
+        j_r, g_r = 1 + jnp.maximum(r, 0) // KV_HEADS, lax.rem(r + KV_HEADS, KV_HEADS)
+
+        @pl.when((r >= 0) & (r < (FWD - 1) * KV_HEADS) & last & sent_ahead(j_r))
+        def _():
+            send(j_r, g_r, j_r + 1, j_r, ahead)
 
         f = t - lag
-
-        @pl.when((f >= 0) & (f < FWD * KV_HEADS))
-        def _():
-            j, g = 1 + f // KV_HEADS, lax.rem(f, KV_HEADS)
-            arrive(j, g)
-
-            @pl.when(j < FWD)
-            def _():
-                send(j, g, j + 1, j, ahead)
-
-            share(j, g)
+        j_f, g_f = 1 + jnp.maximum(f, 0) // KV_HEADS, lax.rem(f + 2 * KV_HEADS, KV_HEADS)
+
+        @pl.when((f >= 0) & ((j_f <= FWD) | ((j_f == FWD + 1) & last)) & live(chip, j_f))
+        def _():
+            arrive(j_f, g_f)
+
+            @pl.when(sent_ahead(j_f) & jnp.logical_not(last))
+            def _():
+                send(j_f, g_f, j_f + 1, j_f, ahead)
+
+            share(j_f, g_f)
 
         @pl.when(t < KV_HEADS)
         def _():
@@ -234,15 +266,17 @@
             v = jnp.maximum(u, 0)
             j = jnp.where(r == 0, REACH - 1 - v // KV_HEADS, 1 + v // KV_HEADS)
             g = lax.rem(v, KV_HEADS)
-
-            @pl.when((u >= 0) & (u < jnp.where(r == 0, BACK, FWD) * KV_HEADS))
+            turned = last & (j == FWD + 1)
+            mine_here = jnp.where(r == 0, (j > FWD) & jnp.logical_not(turned), (j <= FWD) | turned)
+
+            @pl.when((u >= 0) & mine_here & real(chip, j))
             def _():
                 arrive(REACH + j + core, g)
                 attend((j, REACH + j + core), g)
 
             return carry
 
-        @pl.when((t >= KV_HEADS) & (t < 2 * KV_HEADS))
+        @pl.when((t >= KV_HEADS) & (t < 2 * KV_HEADS) & ((core == 1) | real(chip, REACH)))
         def _():
             slot = 2 * REACH - (REACH - 1) * core
             arrive(slot, t - KV_HEADS)
@@ -251,7 +285,7 @@
         lax.fori_loop(0, 2, source, 0)
         return carry
 
-    lax.fori_loop(0, BACK * KV_HEADS + 2, tick, 0)
+    lax.fori_loop(0, BACK * KV_HEADS + 3, tick, 0)
 
     def finish(h, carry):
         g, i = h // GROUP, lax.rem(h, GROUP)
@@ -264,17 +298,21 @@
     lax.fori_loop(0, Q_HEADS, finish, 0)
 
     def drain(i, carry):
-        row = i // KV_HEADS
-        g = lax.rem(i, KV_HEADS)
-        moved(0, g, 1, row, other).wait_send()
-
-        @pl.when(g == 0)
-        def _():
-            moved_seg(0, 1, row, other).wait_send()
+        row, g = i // KV_HEADS, lax.rem(i, KV_HEADS)
+        sent = jnp.where(row < 4, sent_ahead(row), jnp.where(row < 8, sent_behind(REACH + 4 - row), jnp.where(
+            row == 8, live(chip + REACH, REACH), real(chip, row - 9 + core))))
+
+        @pl.when(sent)
+        def _():
+            moved(0, g, 1, row, other).wait_send()
+
+            @pl.when(g == 0)
+            def _():
+                moved_seg(0, 1, row, other).wait_send()
 
         return carry
 
-    lax.fori_loop(0, 16 * KV_HEADS, drain, 0)
+    lax.fori_loop(0, 17 * KV_HEADS, drain, 0)
 
 
 def on_device(queries, key_rows, value_rows, segments):
@@ -297,13 +335,13 @@
             pltpu.VMEM((4, 2 * TOK, TOK), jnp.float32),
             pltpu.SemaphoreType.DMA((2 * KV_HEADS + 2,)),
             pltpu.SemaphoreType.DMA((SLOTS, KV_HEADS)),
-            pltpu.SemaphoreType.DMA((16, KV_HEADS)),
+            pltpu.SemaphoreType.DMA((17, KV_HEADS)),
             pltpu.SemaphoreType.DMA((SLOTS,)),
-            pltpu.SemaphoreType.DMA((16,)),
+            pltpu.SemaphoreType.DMA((17,)),
         ],
         compiler_params=pltpu.CompilerParams(
             collective_id=0, has_side_effects=True, vmem_limit_bytes=30 * 1024 * 1024),
-    )(*(pltpu.with_memory_space_constraint(a, pltpu.HBM) for a in (queries, key_rows, value_rows)), segments.reshape(1, TOK))
+    )(*(pltpu.with_memory_space_constraint(a, pltpu.HBM) for a in (queries, key_rows, value_rows, segments.reshape(1, TOK))))
 
 
 def solution(mesh):

time: 75.5 us -> 73.3 us (0.971)
  the two profiles are of different devices: /device:TPU:1 before, /device:TPU:35 now
where the time goes in v4:
time: 73.3 us; the launch traced here: 73.2 us
  Pallas kernels  71 us (97%)
  local copies, waits for them, and re-layouts  1.58 us (2%)
    pallas_call x1, Pallas kernels, on_device(): pl.pallas_call(kernel, out_shape=(jax.ShapeDtypeStruct((TOK, Q_HEADS * HE...  71 us
    unnamed x2, local copies, waits for them, and re-layouts  1.58 us

profile of v4, /device:TPU:35, one launch (start us, length us, event | category | flops | bytes accessed | tf_op | source)
XLA Modules:
  0.0 73.2 jit_solution(6420838061250809129)
XLA Ops:
  0.6 71.0 %shard_map.59 = (bf16[256,2048]{1,0:T(8,128)(2,1)S(1)}, f32[16,256]{1,0:T(8,128)S(1)}) custom-call(bf16[256,2048]{1,0:T(8,128)(2,1)} %q_hbm.1, bf16[256,512]{1,0:T(8,128)(2,1)} %k_hbm.1, bf16[256,512]{1,0:T(8,128)(2,1)} %v_hbm.1, s32[1,256]{1,0:T(1,128)} %bitcast.1), custom_call_target="tpu_custom_call" | custom-call | tf_op jit(solution)/shard_map/pallas_call | solution.py:319
  71.7 1.0 %copy.8 = bf16[256,2048]{1,0:T(8,128)(2,1)} copy(bf16[256,2048]{1,0:T(8,128)(2,1)S(1)} %get-tuple-element.4) | data formatting | bytes 2097152
  72.6 0.6 copy.9

commit v5 on v4

--- a/solution.py
+++ b/solution.py
@@ -201,6 +201,20 @@
 
     lag = jnp.where(first, 6, jnp.where(z == 1, 3, 1))
 
+    def drain(rows, shared):
+        for row in rows:
+            sent = sent_ahead(row) if row < 4 else sent_behind(REACH + 4 - row) if row < 8 else live(chip + REACH, REACH)
+            drain_row(row, sent)
+        for j in shared:
+            drain_row(9 + j - core, real(chip, j))
+
+    def drain_row(row, sent):
+        @pl.when(sent)
+        def _():
+            moved_seg(0, 1, row, other).wait_send()
+            for g in range(KV_HEADS):
+                moved(0, g, 1, row, other).wait_send()
+
     def tick(t, carry):
         @pl.when((t < KV_HEADS) & live(chip, REACH))
         def _():
@@ -283,36 +297,27 @@
             attend((slot,), t - KV_HEADS)
 
         lax.fori_loop(0, 2, source, 0)
+
+        @pl.when(t == 14)
+        def _():
+            drain((0, 1, 4, 5, 8), (1, 2, 6, 7))
+            drain_row(9 + (REACH - 1) * core, jnp.where(core == 1, real(chip, REACH), chip >= 0))
+
         return carry
 
     lax.fori_loop(0, BACK * KV_HEADS + 3, tick, 0)
 
-    def finish(h, carry):
-        g, i = h // GROUP, lax.rem(h, GROUP)
-        total = acc[g, i, HEAD_DIM:HEAD_DIM + 1, :]
-        part = acc[g, i, :HEAD_DIM, :] / total
-        out_ref[:, pl.ds(pl.multiple_of(h * HEAD_DIM, HEAD_DIM), HEAD_DIM)] = part.T.astype(jnp.bfloat16)
-        lse_ref[pl.ds(h, 1), :] = top[g, i] * SCALE + jnp.log(total)
+    def finish(g, carry):
+        for i in range(GROUP):
+            h = g * GROUP + i
+            total = acc[g, i, HEAD_DIM:HEAD_DIM + 1, :]
+            part = acc[g, i, :HEAD_DIM, :] / total
+            out_ref[:, pl.ds(pl.multiple_of(h * HEAD_DIM, HEAD_DIM), HEAD_DIM)] = part.T.astype(jnp.bfloat16)
+            lse_ref[pl.ds(h, 1), :] = top[g, i] * SCALE + jnp.log(total)
         return carry
 
-    lax.fori_loop(0, Q_HEADS, finish, 0)
-
-    def drain(i, carry):
-        row, g = i // KV_HEADS, lax.rem(i, KV_HEADS)
-        sent = jnp.where(row < 4, sent_ahead(row), jnp.where(row < 8, sent_behind(REACH + 4 - row), jnp.where(
-            row == 8, live(chip + REACH, REACH), real(chip, row - 9 + core))))
-
-        @pl.when(sent)
-        def _():
-            moved(0, g, 1, row, other).wait_send()
-
-            @pl.when(g == 0)
-            def _():
-                moved_seg(0, 1, row, other).wait_send()
-
-        return carry
-
-    lax.fori_loop(0, 17 * KV_HEADS, drain, 0)
+    lax.fori_loop(0, KV_HEADS, finish, 0)
+    drain((2, 3, 6, 7), (3, 4, 5))
 
 
 def on_device(queries, key_rows, value_rows, segments):

time: 73.3 us -> 70.3 us (0.959)
  Pallas kernels: 71 us -> 68 us
    pallas_call x1, Pallas kernels: 71 us -> 68 us  [on_device(): pl.pallas_call(kernel, out_shape=(jax.ShapeDtypeStruct((TOK, Q_HEADS * HE...]
where the time goes in v5:
time: 70.3 us; the launch traced here: 70.2 us
  Pallas kernels  68 us (97%)
  local copies, waits for them, and re-layouts  1.58 us (2%)
    pallas_call x1, Pallas kernels, on_device(): pl.pallas_call(kernel, out_shape=(jax.ShapeDtypeStruct((TOK, Q_HEADS * HE...  68 us
    unnamed x2, local copies, waits for them, and re-layouts  1.58 us

profile of v5, /device:TPU:35, one launch (start us, length us, event | category | flops | bytes accessed | tf_op | source)
XLA Modules:
  0.0 70.2 jit_solution(6823463379882564196)
XLA Ops:
  0.6 68.0 %shard_map.59 = (bf16[256,2048]{1,0:T(8,128)(2,1)S(1)}, f32[16,256]{1,0:T(8,128)S(1)}) custom-call(bf16[256,2048]{1,0:T(8,128)(2,1)} %q_hbm.1, bf16[256,512]{1,0:T(8,128)(2,1)} %k_hbm.1, bf16[256,512]{1,0:T(8,128)(2,1)} %v_hbm.1, s32[1,256]{1,0:T(1,128)} %bitcast.1), custom_call_target="tpu_custom_call" | custom-call | tf_op jit(solution)/shard_map/pallas_call | solution.py:324
  68.6 1.0 %copy.8 = bf16[256,2048]{1,0:T(8,128)(2,1)} copy(bf16[256,2048]{1,0:T(8,128)(2,1)S(1)} %get-tuple-element.4) | data formatting | bytes 2097152
  69.6 0.6 copy.9
